TPU v7x, 256 devices: a whole 4x4x8 slice. The times are simulated.
256 devices in a mesh: seq: 64 (over y_hi, x, z), mp: 4 (over y_lo, core).
Axes of the slice: x: 4, y: 4 (y_hi: 2, y_lo: 2; y = y_hi * 2 + y_lo), z: 8, core: 2. Of those that a mesh axis runs over, the one named last changes fastest.
Arguments:
- tokens: bfloat16 [256, 3584], P('mp'), may hold values from -6 to 6
- gain_attn: float32 [3584], replicated, may hold values from 0.25 to 1.75
- w_query: bfloat16 [3584, 3584], P(None, 'seq'), may hold values from -0.09375 to 0.09375
- query_bias: float32 [3584], P('seq'), may hold values from -3 to 3
- cache_keys: bfloat16 [4, 65536, 128], P(None, 'seq'), may hold values from -80 to 80
- cache_values: bfloat16 [4, 65536, 128], P(None, 'seq'), may hold values from -6 to 6
- w_out: bfloat16 [3584, 3584], P(None, 'seq'), may hold values from -0.09375 to 0.09375
- gain_ffn: float32 [3584], P('seq'), may hold values from 0.25 to 1.75
- w_gate: bfloat16 [3584, 18944], P('mp', 'seq'), may hold values from -0.09375 to 0.09375
- w_up: bfloat16 [3584, 18944], P('mp', 'seq'), may hold values from -0.09375 to 0.09375
- w_down: bfloat16 [18944, 3584], P('seq', 'mp'), may hold values from -0.125 to 0.125
Outputs:
- attended: bfloat16 [256, 3584], P('mp', 'seq')
- layer_out: bfloat16 [256, 3584], P('mp', 'seq')
All inputs are finite; a program needn't handle non-finite values.
Results may differ from a plain program's by a relative error of at most 0.012.
The roundings to bfloat16 on the way count: a program that leaves them out, or rounds other values in their place, can miss the bound.
Values may be sent and summed in bfloat16 or wider, within the bound.
A program may use at most 64 MiB of HBM per device.

v0:
```python
import functools
import math

import jax
import jax.numpy as jnp
from jax import lax
from jax.experimental import pallas as pl
from jax.experimental.pallas import tpu as pltpu
from jax.sharding import PartitionSpec as P

D = 3584
HEAD = 128
GROUP = 7
KV = 4
CTX = 1024
SEQ = 64
MP = 4
TOK = 64
ALL = TOK * MP
COL = 56
FEAT = D // MP
PEER = FEAT // COL
HID = 296
QUART = 80
HIDP = QUART * MP
PK = 32
EPS = 1e-06
MESH = pl.DeviceIdType.MESH
BF = jnp.bfloat16
F32 = jnp.float32
LOG2E = 1.0 / math.log(2.0)


def dot(a, b, dims=((1,), (0,))):
    return lax.dot_general(a, b, (dims, ((), ())), preferred_element_type=F32)


def low_lanes(rows):
    return lax.broadcasted_iota(jnp.int32, (rows, 128), 1) < 64


def row_ids(rows):
    return lax.broadcasted_iota(jnp.int32, (rows, 128), 0)


def swap(x):
    return pltpu.roll(x, 64, axis=1)


def column_of(row):
    n = row.shape[1]
    same = lax.broadcasted_iota(jnp.int32, (n, n), 0) == lax.broadcasted_iota(jnp.int32, (n, n), 1)
    return jnp.sum(jnp.where(same, jnp.broadcast_to(row, (n, n)), 0.0), axis=1, keepdims=True)


def split3(x):
    first = x.astype(BF).astype(F32)
    rest = x - first
    second = rest.astype(BF).astype(F32)
    return first, second, rest - second


def three_rows(x, rows, base=0):
    first, second, third = split3(x)
    at = lax.broadcasted_iota(jnp.int32, (rows, x.shape[1]), 0) - base
    return jnp.where(at == 0, first, jnp.where(at == 1, second, jnp.where(at == 2, third, 0.0)))


def kernel(
    tokens_h, gain_attn_h, wq_h, bias_h, keys_h, values_h, wo_h, gain_ffn_h, wg_h, wu_h, wd_h,
    att_out, lay_out,
    tokens, gain_attn, wq, bias, keys, values, wo, gain_ffn, wg, wu, wd,
    normed, value_t, wd_t, hid_t, work, outs, lsplit, stage1, stage2, stage4, stage6,
    buf1, buf2, buf3, buf4, buf6, la, lb, att3, gu, gstage, gbuf, act, res,
    in_sem, ssem, rsem, asem,
):
    s = lax.axis_index("seq")
    m = lax.axis_index("mp")
    own_m = s // PEER
    own_j = lax.rem(s, PEER)
    mine = own_m == m

    pairs = (
        (tokens_h, tokens), (gain_attn_h, gain_attn), (wq_h, wq), (bias_h, bias),
        (keys_h.at[m], keys), (values_h.at[m], values), (wo_h, wo), (gain_ffn_h, gain_ffn),
        (wg_h, wg), (wu_h, wu), (wd_h, wd.at[pl.ds(0, HID)]),
    )
    loads = [pltpu.make_async_copy(a, b, in_sem.at[i]) for i, (a, b) in enumerate(pairs)]
    for load in loads:
        load.start()

    bar = pltpu.get_barrier_semaphore()

    def greet(p, q):
        pl.semaphore_signal(bar, inc=1, device_id=(p, q), device_id_type=MESH)

    def greet_all(i, c):
        j, q = i // MP, lax.rem(i, MP)

        @pl.when(jnp.logical_not(jnp.logical_and(PEER * m + j == s, q == m)))
        def _():
            greet(PEER * m + j, q)

        @pl.when(jnp.logical_not(jnp.logical_and(i == s, own_m == m)))
        def _():
            greet(i, own_m)

        @pl.when(i != s)
        def _():
            greet(i, m)

        return c

    lax.fori_loop(0, SEQ, greet_all, 0)
    for d in range(1, MP):
        greet(s, lax.rem(m + d, MP))

    loads[0].wait()
    loads[1].wait()
    normed[pl.ds(TOK, TOK), :] = jnp.zeros((TOK, D), BF)

    def norm_rows(i, c):
        at = pl.multiple_of(i * 16, 16)
        x = tokens[pl.ds(at, 16), :].astype(F32)
        mean_sq = jnp.sum(x * x, axis=1, keepdims=True) * (1.0 / D)
        normed[pl.ds(at, 16), :] = (x * lax.rsqrt(mean_sq + EPS) * gain_attn[...]).astype(BF)
        return c

    lax.fori_loop(0, TOK // 16, norm_rows, 0)
    loads[2].wait()
    loads[3].wait()
    q_t = dot(wq[...], normed[...], ((1,), (1,))) + column_of(bias[...])
    low32 = low_lanes(PK)

    def packed(x):
        hi = jnp.concatenate([x[PK:COL], jnp.zeros((8, 128), F32)], axis=0)
        return jnp.where(low32, x[0:PK], swap(hi))

    stage1[...] = packed(q_t).astype(BF)
    pl.semaphore_wait(bar, jnp.where(mine, 2 * SEQ - 2, 2 * SEQ) + SEQ - 1 + MP - 1)

    slot1 = own_j * MP + m

    def gather_to_users(stage, buf, k):
        def send(i, c):
            p = lax.rem(s + i, SEQ)
            local = jnp.logical_and(p == s, mine)

            @pl.when(local)
            def _():
                pltpu.make_async_copy(stage, buf.at[slot1], rsem.at[k]).start()

            @pl.when(jnp.logical_not(local))
            def _():
                pltpu.make_async_remote_copy(
                    src_ref=stage, dst_ref=buf.at[slot1], send_sem=ssem.at[k], recv_sem=rsem.at[k],
                    device_id=(p, own_m), device_id_type=MESH,
                ).start()

            return c

        lax.fori_loop(1, SEQ + 1, send, 0)

    def scatter_to_owners(stage, buf, k):
        def send(i, c):
            at = lax.rem(own_j * MP + m + i, SEQ)
            j, q = at // MP, lax.rem(at, MP)
            p = PEER * m + j
            local = jnp.logical_and(p == s, q == m)

            @pl.when(local)
            def _():
                pltpu.make_async_copy(stage.at[at], buf.at[s], rsem.at[k]).start()

            @pl.when(jnp.logical_not(local))
            def _():
                pltpu.make_async_remote_copy(
                    src_ref=stage.at[at], dst_ref=buf.at[s], send_sem=ssem.at[k], recv_sem=rsem.at[k],
                    device_id=(p, q), device_id_type=MESH,
                ).start()

            return c

        lax.fori_loop(1, SEQ + 1, send, 0)

    def arrived(buf, k):
        pltpu.make_async_copy(buf, buf, rsem.at[k]).wait()

    def sent(buf, k):
        @pl.when(mine)
        def _():
            some = buf.at[pl.ds(0, SEQ - 1)]
            pltpu.make_async_copy(some, some, ssem.at[k]).wait()

        @pl.when(jnp.logical_not(mine))
        def _():
            pltpu.make_async_copy(buf, buf, ssem.at[k]).wait()

    gather_to_users(stage1, buf1, 0)

    first = lax.broadcasted_iota(jnp.int32, (COL, D), 1) - lax.broadcasted_iota(jnp.int32, (COL, D), 0)
    pick = jnp.where(first == s * COL, 1.0, 0.0).astype(BF)
    loads[5].wait()
    value_t[...] = values[...].T
    normed[pl.ds(0, TOK), :] = tokens[...]
    hid_t[...] = dot(pick, normed[...], ((1,), (1,)))
    loads[10].wait()
    wd[pl.ds(HID, HIDP - HID), :] = jnp.zeros((HIDP - HID, FEAT), BF)
    wd_t[...] = wd[...].T
    outs[pl.ds(FEAT, 8), :] = jnp.zeros((8, ALL), F32)
    gu[:, pl.ds(HID, HIDP - HID), :] = jnp.zeros((2, HIDP - HID, ALL), F32)
    for i in (4, 6, 7, 8, 9):
        loads[i].wait()

    def unpack_chunks(buf, squares):
        def one(j, sums):
            sums = list(sums)
            for t in range(2):
                a = buf[j * MP + 2 * t].astype(F32)
                b = buf[j * MP + 2 * t + 1].astype(F32)
                lo = jnp.where(low32, a, swap(b))
                hi = jnp.where(low32, swap(a), b)
                at = pl.multiple_of(j * COL, 8)
                work[pl.ds(at, PK), pl.ds(128 * t, 128)] = lo
                work[pl.ds(pl.multiple_of(at + PK, 8), COL - PK), pl.ds(128 * t, 128)] = hi[0 : COL - PK]
                if squares:
                    sums[t] = sums[t] + hi[COL - PK : PK]
            return tuple(sums)

        zero = jnp.zeros((8, 128), F32)
        return lax.fori_loop(0, PEER, one, (zero, zero))

    def pack_chunks(stage, stats):
        def one(j, c):
            at = pl.multiple_of(j * COL, 8)
            for t in range(2):
                r = outs[pl.ds(at, 2 * PK), pl.ds(128 * t, 128)]
                lo, hi = r[0:PK], r[PK : 2 * PK]
                a = jnp.where(low32, lo, swap(hi))
                b = jnp.where(low32, swap(lo), hi)
                if stats:
                    h0, h1 = (j * COL) // HEAD, (j * COL + COL - 1) // HEAD
                    low8 = low_lanes(8)
                    both = jnp.where(
                        row_ids(8) < 3, lsplit[h0, :, pl.ds(128 * t, 128)], lsplit[h1, :, pl.ds(128 * t, 128)]
                    )
                    a = jnp.concatenate([a[0:24], jnp.where(low8, a[24:PK], swap(both))], axis=0)
                    b = jnp.concatenate([b[0:24], jnp.where(low8, b[24:PK], both)], axis=0)
                stage[j * MP + 2 * t] = a.astype(BF)
                stage[j * MP + 2 * t + 1] = b.astype(BF)
            return c

        lax.fori_loop(0, PEER, one, 0)

    arrived(buf1, 0)
    unpack_chunks(buf1, False)
    scale = HEAD ** (-0.5) * LOG2E

    def one_head(h, c):
        at = pl.multiple_of(h * HEAD, HEAD)
        scores = dot(keys[...], work[pl.ds(at, HEAD), :].astype(BF)) * scale
        top = jnp.max(scores, axis=0, keepdims=True)
        probs = jnp.exp2(scores - top)
        total = jnp.sum(probs, axis=0, keepdims=True)
        outs[pl.ds(at, HEAD), :] = dot(value_t[...], probs.astype(BF)) * (1.0 / total)
        level = top + jnp.log(total) * LOG2E
        lsplit[h] = three_rows(level, 8) + three_rows(level, 8, 3)
        return c

    lax.fori_loop(0, GROUP, one_head, 0)
    pack_chunks(stage2, True)
    scatter_to_owners(stage2, buf2, 1)

    arrived(buf2, 1)
    low128 = low_lanes(SEQ)

    def levels(i, c):
        part = buf2[i, pl.ds(16, 16), :].astype(F32)[8:16]
        at = row_ids(8)
        la[pl.ds(i, 1), :] = jnp.sum(jnp.where(at < 3, part, 0.0), axis=0, keepdims=True)
        lb[pl.ds(i, 1), :] = jnp.sum(
            jnp.where(jnp.logical_and(at >= 3, at < 6), part, 0.0), axis=0, keepdims=True
        )
        return c

    lax.fori_loop(0, SEQ, levels, 0)
    for ref in (la, lb):
        level = ref[...]
        level = jnp.where(low128, swap(level), level)
        weight = jnp.exp2(level - jnp.max(level, axis=0, keepdims=True))
        ref[...] = weight / jnp.sum(weight, axis=0, keepdims=True)
    edge = HEAD * ((own_j * COL) // HEAD + 1) - own_j * COL
    first_head = row_ids(PK) + jnp.where(low32, 0, PK) < edge

    def combine(i, acc):
        return acc + buf2[i].astype(F32) * jnp.where(first_head, la[pl.ds(i, 1), :], lb[pl.ds(i, 1), :])

    merged = lax.fori_loop(0, SEQ, combine, jnp.zeros((PK, 128), F32)).astype(BF)
    buf3[s] = merged

    def send3(i, c):
        pltpu.make_async_remote_copy(
            src_ref=buf3.at[s], dst_ref=buf3.at[s], send_sem=ssem.at[2], recv_sem=rsem.at[2],
            device_id=(lax.rem(s + i, SEQ), m), device_id_type=MESH,
        ).start()
        return c

    lax.fori_loop(1, SEQ, send3, 0)

    def unpacked(x, out):
        out[pl.ds(0, PK), :] = x[:, 0:64].astype(BF)
        out[pl.ds(PK, COL - PK), :] = swap(x)[0 : COL - PK, 0:64].astype(BF)

    unpacked(merged.astype(F32), att_out)
    res_hid = packed(hid_t[...])
    gain_pk = packed(jnp.broadcast_to(column_of(gain_ffn[...]), (COL, 128)))
    gain_pk = jnp.where(low32, gain_pk, packed(swap(jnp.broadcast_to(column_of(gain_ffn[...]), (COL, 128)))))
    others = buf3.at[pl.ds(0, SEQ - 1)]
    pltpu.make_async_copy(others, others, rsem.at[2]).wait()

    def spread(i, c):
        x = buf3[i].astype(F32)
        at = pl.multiple_of(i * COL, 8)
        att3[pl.ds(at, PK), :] = x
        att3[pl.ds(pl.multiple_of(at + PK, 8), COL - PK), :] = swap(x)[0 : COL - PK]
        return c

    lax.fori_loop(0, SEQ, spread, 0)
    projected = jnp.zeros((COL, 128), F32)
    for i in range(4):
        projected += dot(wo[:, pl.ds(i * FEAT, FEAT)], att3[pl.ds(i * FEAT, FEAT), :].astype(BF))
    residual = res_hid + packed(projected)
    res[...] = residual

    real = jnp.logical_or(low32, row_ids(PK) < COL - PK)
    squares = jnp.sum(jnp.where(real, residual * residual, 0.0), axis=0, keepdims=True)
    squares = squares + swap(squares)
    scaled = residual * gain_pk
    stage4[...] = jnp.where(real, scaled, three_rows(squares, PK, 24)).astype(BF)
    gather_to_users(stage4, buf4, 3)
    arrived(buf4, 3)
    sums = unpack_chunks(buf4, True)
    sq = jnp.concatenate([jnp.sum(x, axis=0, keepdims=True) for x in sums], axis=1)

    features = work[pl.ds(0, FEAT), :].astype(BF)
    gu[0, pl.ds(0, HID), :] = dot(wg[...], features)
    gu[1, pl.ds(0, HID), :] = dot(wu[...], features)
    sq_rows = three_rows(sq, 16).astype(BF)
    for d in range(1, MP):
        q = lax.rem(m + d, MP)
        at = pl.multiple_of(q * QUART, 16)
        gstage[d, pl.ds(0, QUART), :] = gu[0, pl.ds(at, QUART), :].astype(BF)
        gstage[d, pl.ds(QUART, QUART), :] = gu[1, pl.ds(at, QUART), :].astype(BF)
        gstage[d, pl.ds(2 * QUART, 16), :] = sq_rows
        pltpu.make_async_remote_copy(
            src_ref=gstage.at[d], dst_ref=gbuf.at[d], send_sem=asem.at[0, d], recv_sem=asem.at[1, d],
            device_id=(s, q), device_id_type=MESH,
        ).start()
    at = pl.multiple_of(m * QUART, 16)
    gate = gu[0, pl.ds(at, QUART), :]
    up = gu[1, pl.ds(at, QUART), :]
    for d in range(1, MP):
        pltpu.make_async_copy(gbuf.at[d], gbuf.at[d], asem.at[1, d]).wait()
        gate += gbuf[d, pl.ds(0, QUART), :].astype(F32)
        up += gbuf[d, pl.ds(QUART, QUART), :].astype(F32)
        sq += jnp.sum(gbuf[d, pl.ds(2 * QUART, 16), :].astype(F32), axis=0, keepdims=True)
    factor = lax.rsqrt(sq * (1.0 / D) + EPS)
    gate = gate * factor
    up = up * factor
    act[pl.ds(at, QUART), :] = (gate / (1.0 + jnp.exp(-gate)) * up).astype(BF)
    for d in range(1, MP):
        q = lax.rem(m + d, MP)
        pltpu.make_async_remote_copy(
            src_ref=act.at[pl.ds(at, QUART)], dst_ref=act.at[pl.ds(at, QUART)],
            send_sem=asem.at[2, d], recv_sem=asem.at[3, d], device_id=(s, q), device_id_type=MESH,
        ).start()
    for d in range(1, MP):
        src = act.at[pl.ds(pl.multiple_of(lax.rem(m + MP - d, MP) * QUART, 16), QUART)]
        pltpu.make_async_copy(src, src, asem.at[3, d]).wait()

    outs[pl.ds(0, FEAT), :] = dot(wd_t[...], act[...])
    pack_chunks(stage6, False)
    scatter_to_owners(stage6, buf6, 4)
    arrived(buf6, 4)

    def add(i, acc):
        return acc + buf6[i].astype(F32)

    unpacked(lax.fori_loop(0, SEQ, add, res[...]), lay_out)

    for k, buf in ((0, buf1), (1, buf2), (3, buf4), (4, buf6)):
        sent(buf, k)
    pltpu.make_async_copy(others, others, ssem.at[2]).wait()
    for d in range(1, MP):
        pltpu.make_async_copy(gstage.at[d], gstage.at[d], asem.at[0, d]).wait()
        src = act.at[pl.ds(at, QUART)]
        pltpu.make_async_copy(src, src, asem.at[2, d]).wait()


def body(tokens, gain_attn, w_query, query_bias, cache_keys, cache_values, w_out, gain_ffn, w_gate, w_up, w_down):
    v = pltpu.VMEM
    chunk = (SEQ, PK, 128)
    scratch = [
        v((TOK, D), BF), v((1, D), F32), v((COL, D), BF), v((1, COL), F32), v((CTX, HEAD), BF), v((CTX, HEAD), BF),
        v((COL, D), BF), v((1, COL), F32), v((HID, FEAT), BF), v((HID, FEAT), BF), v((HIDP, FEAT), BF),
        v((2 * TOK, D), BF),
        v((HEAD, CTX), BF),
        v((FEAT, HIDP), BF),
        v((COL, 128), F32),
        v((FEAT, ALL), F32),
        v((FEAT + 8, ALL), F32),
        v((8, 8, ALL), F32),
        v((PK, 128), BF), v(chunk, BF), v((PK, 128), BF), v(chunk, BF),
        v(chunk, BF), v(chunk, BF), v(chunk, BF), v(chunk, BF), v(chunk, BF),
        v((SEQ, 128), F32), v((SEQ, 128), F32),
        v((D, 128), F32),
        v((2, HIDP, ALL), F32),
        v((MP, 2 * QUART + 16, ALL), BF), v((MP, 2 * QUART + 16, ALL), BF),
        v((HIDP, ALL), BF),
        v((PK, 128), F32),
        pltpu.SemaphoreType.DMA((11,)),
        pltpu.SemaphoreType.DMA((5,)),
        pltpu.SemaphoreType.DMA((5,)),
        pltpu.SemaphoreType.DMA((4, MP)),
    ]
    any_space = pl.BlockSpec(memory_space=pl.ANY)
    attended, layer = pl.pallas_call(
        kernel,
        out_shape=(jax.ShapeDtypeStruct((COL, TOK), BF), jax.ShapeDtypeStruct((COL, TOK), BF)),
        in_specs=[any_space] * 11,
        out_specs=(pl.BlockSpec(memory_space=pltpu.VMEM), pl.BlockSpec(memory_space=pltpu.VMEM)),
        scratch_shapes=scratch,
        compiler_params=pltpu.CompilerParams(
            collective_id=0, has_side_effects=True, vmem_limit_bytes=48 * 1024 * 1024
        ),
        name="layer",
    )(
        tokens, gain_attn.reshape(1, D), w_query.T, query_bias.reshape(1, COL), cache_keys, cache_values,
        w_out.T, gain_ffn.reshape(1, COL), w_gate.T, w_up.T, w_down,
    )
    return attended.T, layer.T


def solution(mesh):
    placed = (
        P("mp", None), P(), P(None, "seq"), P("seq"), P(None, "seq", None), P(None, "seq", None),
        P(None, "seq"), P("seq"), P("mp", "seq"), P("mp", "seq"), P("seq", "mp"),
    )
    return jax.shard_map(
        body, mesh=mesh, in_specs=placed, out_specs=(P("mp", "seq"), P("mp", "seq")), check_vma=False
    )
```

profile of v0, /device:TPU:1, one launch (start us, length us, event | category | flops | bytes accessed | tf_op | source)
XLA Modules:
  0.0 128.7 jit_solution(3250642079600253881)
XLA Ops:
  0.6 0.0 copy-start.8
  0.6 0.0 copy-start.9
  0.7 0.7 reshape.13.gain_attn_h
  1.4 0.0 copy-done.8
  1.4 0.0 copy-done.9
  1.4 0.0 copy-start
  1.4 1.2 copy-done
  2.6 0.0 copy-start.1
  2.6 1.2 copy-done.1
  3.9 0.0 copy-start.2
  3.9 1.0 copy-done.2
  4.9 0.0 copy-start.3
  4.9 1.0 copy-done.3
  6.0 0.0 copy-start.4
  6.0 1.0 copy-done.4
  7.0 0.0 copy-start.5
  7.0 1.0 copy-done.5
  8.0 0.0 copy-start.6
  8.0 1.0 copy-done.6
  9.0 0.0 copy-start.7
  9.0 1.0 copy-done.7
  10.0 117.5 %layer.1 = (bf16[56,64]{1,0:T(8,128)(2,1)S(1)}, bf16[56,64]{1,0:T(8,128)(2,1)S(1)}) custom-call(bf16[64,3584]{1,0:T(8,128)(2,1)S(1)} %copy-done.5, f32[1,3584]{1,0:T(1,128)S(1)} %reshape.13.gain_attn_h, bf16[56,3584]{1,0:T(8,128)(2,1)S(1)} %bitcast.10, f32[1,56]{1,0:T(1,128)S(1)} %bitcast.14, bf16[4,1024,128]{2,1,0:T(8,128)(2,1)S(1)} %copy-done, ...), custom_call_target="tpu_custom_call" | custom-call | tf_op jit(solution)/shard_map/layer/pallas_call | solution.py:427
  127.5 0.6 copy.15
  128.1 0.6 copy.16
Async XLA Ops:
  0.6 0.8 copy-start.8
  0.6 0.8 copy-start.9
  1.4 1.2 copy-start
  2.6 1.2 copy-start.1
  3.9 1.0 copy-start.2
  4.9 1.0 copy-start.3
  6.0 1.0 copy-start.4
  7.0 1.0 copy-start.5
  8.0 1.0 copy-start.6
  9.0 1.0 copy-start.7
where the time goes:
time: 129 us
  Pallas kernels  117 us (91%)
  local copies, waits for them, and re-layouts  10.5 us (8%)
    pallas_call x1, Pallas kernels, body(): pl.pallas_call(kernel, out_shape=(jax.ShapeDtypeStruct((COL, TOK), BF), j...  117 us
    unnamed x22, local copies, waits for them, and re-layouts  9.8 us

commit v1 on v0

v1 whole, which is shorter than its diff:
```python
import functools
import math

import jax
import jax.numpy as jnp
from jax import lax
from jax.experimental import pallas as pl
from jax.experimental.pallas import tpu as pltpu
from jax.sharding import PartitionSpec as P

D = 3584
HEAD = 128
GROUP = 7
KV = 4
CTX = 1024
SEQ = 64
MP = 4
TOK = 64
ALL = TOK * MP
COL = 56
FEAT = D // MP
PEER = FEAT // COL
HID = 296
QUART = 80
HIDP = QUART * MP
PK = 32
LINE = 8
EPS = 1e-06
MESH = pl.DeviceIdType.MESH
BF = jnp.bfloat16
F32 = jnp.float32
LOG2E = 1.0 / math.log(2.0)


def dot(a, b, dims=((1,), (0,))):
    return lax.dot_general(a, b, (dims, ((), ())), preferred_element_type=F32)


def low_lanes(rows):
    return lax.broadcasted_iota(jnp.int32, (rows, 128), 1) < 64


def row_ids(rows):
    return lax.broadcasted_iota(jnp.int32, (rows, 128), 0)


def swap(x):
    return pltpu.roll(x, 64, axis=1)


def column_of(row):
    n = row.shape[1]
    same = lax.broadcasted_iota(jnp.int32, (n, n), 0) == lax.broadcasted_iota(jnp.int32, (n, n), 1)
    return jnp.sum(jnp.where(same, jnp.broadcast_to(row, (n, n)), 0.0), axis=1, keepdims=True)


def split3(x):
    first = x.astype(BF).astype(F32)
    rest = x - first
    second = rest.astype(BF).astype(F32)
    return first, second, rest - second


def three_rows(x, rows, base=0):
    first, second, third = split3(x)
    at = lax.broadcasted_iota(jnp.int32, (rows, x.shape[1]), 0) - base
    return jnp.where(at == 0, first, jnp.where(at == 1, second, jnp.where(at == 2, third, 0.0)))


def merge_eight(chunks, j):
    at = row_ids(8)
    high = jnp.logical_not(low_lanes(8))
    sides = ([], [])
    for i in range(8):
        part = chunks[i, 24:PK]
        sides[0].append(jnp.sum(jnp.where(at < 3, part, 0.0), axis=0, keepdims=True))
        sides[1].append(jnp.sum(jnp.where(jnp.logical_and(at >= 3, at < 6), part, 0.0), axis=0, keepdims=True))
    weights, levels = [], []
    for rows in sides:
        level = jnp.concatenate(rows, axis=0)
        level = jnp.where(high, level, swap(level))
        top = jnp.max(level, axis=0, keepdims=True)
        weight = jnp.exp2(level - top)
        total = jnp.sum(weight, axis=0, keepdims=True)
        weights.append(weight / total)
        levels.append(top + jnp.log(total) * LOG2E)
    edge = HEAD * ((j * COL) // HEAD + 1) - j * COL
    first_head = row_ids(PK) + jnp.where(low_lanes(PK), 0, PK) < edge
    acc = jnp.zeros((PK, 128), F32)
    for i in range(8):
        acc += chunks[i] * jnp.where(first_head, weights[0][i : i + 1], weights[1][i : i + 1])
    return acc, levels


def kernel(
    tokens_h, gain_attn_h, wq_h, bias_h, keys_h, values_h, wo_h, gain_ffn_h, wg_h, wu_h, wd_h,
    att_out, lay_out,
    tokens, gain_attn, wq, bias, keys, values, wo, gain_ffn, wg, wu, wd,
    normed, value_t, wd_t, hid_t, wo_e, work, outs, lsplit, stage2, stage6,
    line1, line3, line4, buf1, buf3, buf4, plane2, plane6, rel2, rel6, line2, line6,
    gu, gstage, gbuf, act, res,
    in_sem, zsend, zrecv, psend, precv, rrecv, asem,
):
    s = lax.axis_index("seq")
    m = lax.axis_index("mp")
    own_m = s // PEER
    own_j = lax.rem(s, PEER)
    z = lax.rem(s, LINE)
    line = s - z
    here = s // LINE
    mine = own_m == m
    group = (own_j // LINE) * MP + m

    pairs = (
        (tokens_h, tokens), (gain_attn_h, gain_attn), (wq_h, wq), (bias_h, bias),
        (keys_h.at[m], keys), (values_h.at[m], values), (wo_h, wo), (gain_ffn_h, gain_ffn),
        (wg_h, wg), (wu_h, wu), (wd_h, wd.at[pl.ds(0, HID)]),
    )
    loads = [pltpu.make_async_copy(a, b, in_sem.at[i]) for i, (a, b) in enumerate(pairs)]
    for load in loads:
        load.start()

    bar = pltpu.get_barrier_semaphore()

    def greet(p, q):
        pl.semaphore_signal(bar, inc=1, device_id=(p, q), device_id_type=MESH)

    for d in range(1, LINE):
        greet(line + lax.rem(z + d, LINE), m)
    for g in range(8):
        p, q = PEER * m + LINE * (g // MP) + z, g % MP
        local = jnp.logical_and(p == s, q == m)

        @pl.when(jnp.logical_not(local))
        def _(p=p, q=q):
            greet(p, q)

        @pl.when(jnp.logical_not(jnp.logical_and(here == g, mine)))
        def _(g=g):
            greet(LINE * g + z, own_m)

    for d in range(1, 8):
        greet(LINE * lax.rem(here + d, 8) + z, m)
    for d in range(1, MP):
        greet(s, lax.rem(m + d, MP))

    loads[0].wait()
    loads[1].wait()
    normed[pl.ds(TOK, TOK), :] = jnp.zeros((TOK, D), BF)
    gain_row = jnp.concatenate([gain_attn[i : i + 1, :] for i in range(D // 128)], axis=1)

    def norm_rows(i, c):
        at = pl.multiple_of(i * 16, 16)
        x = tokens[pl.ds(at, 16), :].astype(F32)
        mean_sq = jnp.sum(x * x, axis=1, keepdims=True) * (1.0 / D)
        normed[pl.ds(at, 16), :] = (x * lax.rsqrt(mean_sq + EPS) * gain_row).astype(BF)
        return c

    lax.fori_loop(0, TOK // 16, norm_rows, 0)
    loads[2].wait()
    loads[3].wait()
    q_t = dot(wq[...], normed[...], ((1,), (1,))) + column_of(bias[...])
    low32 = low_lanes(PK)

    def packed(x):
        hi = jnp.concatenate([x[PK:COL], jnp.zeros((8, 128), F32)], axis=0)
        return jnp.where(low32, x[0:PK], swap(hi))

    def along_line(held, k):
        for d in (4, 3, 5, 2, 6, 1, 7):
            pltpu.make_async_remote_copy(
                src_ref=held.at[z], dst_ref=held.at[z], send_sem=zsend.at[k], recv_sem=zrecv.at[k, LINE - d],
                device_id=(line + lax.rem(z + d, LINE), m), device_id_type=MESH,
            ).start()

    def on_to_plane(held, buf, k, target, place, own, first, last):
        def step(i, c):
            e = lax.rem(jnp.where(lax.rem(i, 2) == 1, (i + 1) // 2, LINE - i // 2), LINE)
            at = lax.rem(z + e, LINE)

            @pl.when(i > 0)
            def _():
                pltpu.make_async_copy(held.at[at], held.at[at], zrecv.at[k, e]).wait()

            for d in range(1, 8):
                p = lax.rem(here + d, 8)
                pltpu.make_async_remote_copy(
                    src_ref=held.at[at], dst_ref=buf.at[place, at], send_sem=psend.at[k], recv_sem=precv.at[k],
                    device_id=(LINE * p + z, target), device_id_type=MESH,
                ).start()

            @pl.when(own)
            def _():
                pltpu.make_async_copy(held.at[at], buf.at[place, at], precv.at[k]).start()

            @pl.when(jnp.logical_not(own))
            def _():
                pltpu.make_async_remote_copy(
                    src_ref=held.at[at], dst_ref=buf.at[place, at], send_sem=psend.at[k], recv_sem=precv.at[k],
                    device_id=(s, target), device_id_type=MESH,
                ).start()

            return c

        lax.fori_loop(first, last, step, 0)

    def arrived(buf, sem):
        pltpu.make_async_copy(buf, buf, sem).wait()

    def sent(buf, sem, own):
        @pl.when(own)
        def _():
            arrived(buf.at[pl.ds(0, 7)], sem)

        @pl.when(jnp.logical_not(own))
        def _():
            arrived(buf, sem)

    line1[z] = packed(q_t).astype(BF)
    pl.semaphore_wait(bar, 7 + jnp.where(mine, 14, 16) + 7 + MP - 1)
    along_line(line1, 0)
    on_to_plane(line1, buf1, 0, own_m, group, mine, 0, 1)

    loads[5].wait()
    value_t[...] = values[...].T
    on_to_plane(line1, buf1, 0, own_m, group, mine, 1, LINE)
    first = lax.broadcasted_iota(jnp.int32, (COL, D), 1) - lax.broadcasted_iota(jnp.int32, (COL, D), 0)
    pick = jnp.where(first == s * COL, 1.0, 0.0).astype(BF)
    normed[pl.ds(0, TOK), :] = tokens[...]
    hid_t[...] = dot(pick, normed[...], ((1,), (1,)))
    loads[10].wait()
    wd[pl.ds(HID, HIDP - HID), :] = jnp.zeros((HIDP - HID, FEAT), BF)
    wd_t[...] = wd[...].T
    outs[pl.ds(FEAT, 8), :] = jnp.zeros((8, ALL), F32)
    gu[:, pl.ds(HID, HIDP - HID), :] = jnp.zeros((2, HIDP - HID, ALL), F32)
    wide = PEER * PK
    c_at = lax.broadcasted_iota(jnp.int32, (FEAT, wide), 1)
    r_at = lax.broadcasted_iota(jnp.int32, (FEAT, wide), 0) - COL * (c_at // PK)
    c_at = lax.rem(c_at, PK)
    pick_lo = jnp.where(r_at == c_at, 1.0, 0.0).astype(BF)
    pick_hi = jnp.where(jnp.logical_and(r_at == c_at + PK, c_at < COL - PK), 1.0, 0.0).astype(BF)
    wo_e[...] = jnp.zeros((128, SEQ * PK), BF)
    loads[6].wait()
    for i in range(MP):
        part = wo[:, pl.ds(i * FEAT, FEAT)]
        wo_e[pl.ds(0, COL), pl.ds(i * wide, wide)] = dot(part, pick_lo).astype(BF)
        wo_e[pl.ds(64, COL), pl.ds(i * wide, wide)] = dot(part, pick_hi).astype(BF)
    for i in (4, 7, 8, 9):
        loads[i].wait()

    def unpack_chunks(buf, squares):
        def one(j, sums):
            sums = list(sums)
            for t in range(2):
                a = buf[(j // LINE) * MP + 2 * t, lax.rem(j, LINE)].astype(F32)
                b = buf[(j // LINE) * MP + 2 * t + 1, lax.rem(j, LINE)].astype(F32)
                lo = jnp.where(low32, a, swap(b))
                hi = jnp.where(low32, swap(a), b)
                at = pl.multiple_of(j * COL, 8)
                work[pl.ds(at, PK), pl.ds(128 * t, 128)] = lo
                work[pl.ds(pl.multiple_of(at + PK, 8), COL - PK), pl.ds(128 * t, 128)] = hi[0 : COL - PK]
                if squares:
                    sums[t] = sums[t] + hi[COL - PK : PK]
            return tuple(sums)

        zero = jnp.zeros((8, 128), F32)
        return lax.fori_loop(0, PEER, one, (zero, zero), unroll=4)

    low8 = low_lanes(8)

    def far_first(i):
        return lax.rem(LINE + LINE // 2 + jnp.where(lax.rem(i, 2) == 1, -((i + 1) // 2), i // 2), LINE)

    def to_plane(stage, plane, k, stats):
        def step(i, c):
            e = far_first(i)
            to_z = lax.rem(z + e, LINE)
            for half in range(2):
                j = half * LINE + to_z
                at = pl.multiple_of(j * COL, 8)
                for t in range(2):
                    r = outs[pl.ds(at, 2 * PK), pl.ds(128 * t, 128)]
                    lo, hi = r[0:PK], r[PK : 2 * PK]
                    a = jnp.where(low32, lo, swap(hi))
                    b = jnp.where(low32, swap(lo), hi)
                    if stats:
                        h0, h1 = (j * COL) // HEAD, (j * COL + COL - 1) // HEAD
                        both = jnp.where(
                            row_ids(8) < 3, lsplit[h0, :, pl.ds(128 * t, 128)], lsplit[h1, :, pl.ds(128 * t, 128)]
                        )
                        a = jnp.concatenate([a[0:24], jnp.where(low8, a[24:PK], swap(both))], axis=0)
                        b = jnp.concatenate([b[0:24], jnp.where(low8, b[24:PK], both)], axis=0)
                    stage[to_z, half * MP + 2 * t] = a.astype(BF)
                    stage[to_z, half * MP + 2 * t + 1] = b.astype(BF)
            for g in range(8):
                p, q = PEER * m + LINE * (g // MP) + z, g % MP
                local = jnp.logical_and(p == s, q == m)

                @pl.when(local)
                def _():
                    pltpu.make_async_copy(stage.at[to_z, g], plane.at[to_z, here], rrecv.at[k, e]).start()

                @pl.when(jnp.logical_not(local))
                def _():
                    pltpu.make_async_remote_copy(
                        src_ref=stage.at[to_z, g], dst_ref=plane.at[to_z, here],
                        send_sem=psend.at[k], recv_sem=rrecv.at[k, e], device_id=(p, q), device_id_type=MESH,
                    ).start()

            return c

        lax.fori_loop(0, LINE, step, 0)

    def pass_on(plane, rel, held, k, join):
        def step(i, c):
            e = far_first(i)
            to_z = lax.rem(z + e, LINE)
            arrived(plane.at[to_z], rrecv.at[k, e])
            rel[to_z] = join(plane[to_z].astype(F32), to_z).astype(BF)
            pltpu.make_async_remote_copy(
                src_ref=rel.at[to_z], dst_ref=held.at[z], send_sem=zsend.at[k], recv_sem=zrecv.at[k, 0],
                device_id=(line + to_z, m), device_id_type=MESH,
            ).start()
            return c

        lax.fori_loop(0, LINE - 1, step, 0)
        arrived(plane.at[z], rrecv.at[k, 0])
        held[z] = join(plane[z].astype(F32), z).astype(BF)
        arrived(held.at[pl.ds(0, 7)], zrecv.at[k, 0])

    arrived(buf1, precv.at[0])
    unpack_chunks(buf1, False)
    scale = HEAD ** (-0.5) * LOG2E

    def one_head(h, c):
        at = pl.multiple_of(h * HEAD, HEAD)
        scores = dot(keys[...], work[pl.ds(at, HEAD), :].astype(BF)) * scale
        top = jnp.max(scores, axis=0, keepdims=True)
        probs = jnp.exp2(scores - top)
        total = jnp.sum(probs, axis=0, keepdims=True)
        outs[pl.ds(at, HEAD), :] = dot(value_t[...], probs.astype(BF)) * (1.0 / total)
        level = top + jnp.log(total) * LOG2E
        lsplit[h] = three_rows(level, 8) + three_rows(level, 8, 3)
        return c

    lax.fori_loop(0, GROUP, one_head, 0)

    to_plane(stage2, plane2, 1, True)

    def join2(chunks, to_z):
        value, levels = merge_eight(chunks, (own_j // LINE) * LINE + to_z)
        rows = three_rows(levels[0], 8) + three_rows(levels[1], 8, 3)
        return jnp.concatenate([value[0:24], jnp.where(low8, value[24:PK], rows)], axis=0)

    pass_on(plane2, rel2, line2, 1, join2)
    merged = merge_eight(line2[...].astype(F32), own_j)[0].astype(BF)
    line3[z] = merged

    along_line(line3, 2)
    on_to_plane(line3, buf3, 2, m, here, True, 0, LINE)

    def unpacked(x, out):
        out[pl.ds(0, PK), :] = x[:, 0:64].astype(BF)
        out[pl.ds(PK, COL - PK), :] = swap(x)[0 : COL - PK, 0:64].astype(BF)

    unpacked(merged.astype(F32), att_out)
    res_hid = packed(hid_t[...])
    gain_col = jnp.broadcast_to(column_of(gain_ffn[...]), (COL, 128))
    gain_pk = packed(gain_col)
    arrived(buf3, precv.at[2])
    both = dot(wo_e[...], buf3[...].reshape(SEQ * PK, 128))
    residual = res_hid + packed(both[0:COL] + swap(both[64 : 64 + COL]))
    res[...] = residual

    real = jnp.logical_or(low32, row_ids(PK) < COL - PK)
    squares = jnp.sum(jnp.where(real, residual * residual, 0.0), axis=0, keepdims=True)
    squares = squares + swap(squares)
    scaled = residual * gain_pk
    line4[z] = jnp.where(real, scaled, three_rows(squares, PK, 24)).astype(BF)
    along_line(line4, 3)
    on_to_plane(line4, buf4, 3, own_m, group, mine, 0, LINE)
    arrived(buf4, precv.at[3])
    sums = unpack_chunks(buf4, True)
    sq = jnp.concatenate([jnp.sum(x, axis=0, keepdims=True) for x in sums], axis=1)

    features = work[pl.ds(0, FEAT), :].astype(BF)
    gu[0, pl.ds(0, HID), :] = dot(wg[...], features)
    gu[1, pl.ds(0, HID), :] = dot(wu[...], features)
    sq_rows = three_rows(sq, 16).astype(BF)
    for d in range(1, MP):
        q = lax.rem(m + d, MP)
        at = pl.multiple_of(q * QUART, 16)
        gstage[d, pl.ds(0, QUART), :] = gu[0, pl.ds(at, QUART), :].astype(BF)
        gstage[d, pl.ds(QUART, QUART), :] = gu[1, pl.ds(at, QUART), :].astype(BF)
        gstage[d, pl.ds(2 * QUART, 16), :] = sq_rows
        pltpu.make_async_remote_copy(
            src_ref=gstage.at[d], dst_ref=gbuf.at[d], send_sem=asem.at[0, d], recv_sem=asem.at[1, d],
            device_id=(s, q), device_id_type=MESH,
        ).start()
    at = pl.multiple_of(m * QUART, 16)
    gate = gu[0, pl.ds(at, QUART), :]
    up = gu[1, pl.ds(at, QUART), :]
    for d in range(1, MP):
        arrived(gbuf.at[d], asem.at[1, d])
        gate += gbuf[d, pl.ds(0, QUART), :].astype(F32)
        up += gbuf[d, pl.ds(QUART, QUART), :].astype(F32)
        sq += jnp.sum(gbuf[d, pl.ds(2 * QUART, 16), :].astype(F32), axis=0, keepdims=True)
    factor = lax.rsqrt(sq * (1.0 / D) + EPS)
    gate = gate * factor
    up = up * factor
    act[pl.ds(at, QUART), :] = (gate / (1.0 + jnp.exp(-gate)) * up).astype(BF)
    for d in range(1, MP):
        q = lax.rem(m + d, MP)
        pltpu.make_async_remote_copy(
            src_ref=act.at[pl.ds(at, QUART)], dst_ref=act.at[pl.ds(at, QUART)],
            send_sem=asem.at[2, d], recv_sem=asem.at[3, d], device_id=(s, q), device_id_type=MESH,
        ).start()
    for d in range(1, MP):
        arrived(act.at[pl.ds(pl.multiple_of(lax.rem(m + MP - d, MP) * QUART, 16), QUART)], asem.at[3, d])

    outs[pl.ds(0, FEAT), :] = dot(wd_t[...], act[...])
    to_plane(stage6, plane6, 4, False)
    pass_on(plane6, rel6, line6, 4, lambda chunks, to_z: jnp.sum(chunks, axis=0))
    unpacked(res[...] + jnp.sum(line6[...].astype(F32), axis=0), lay_out)

    for k in range(5):
        arrived(line1.at[pl.ds(0, 7)], zsend.at[k])
    for k, buf in ((0, buf1), (1, plane2), (3, buf4), (4, plane6)):
        sent(buf, psend.at[k], mine)
    arrived(buf3.at[pl.ds(0, 7)], psend.at[2])
    for d in range(1, MP):
        arrived(gstage.at[d], asem.at[0, d])
        arrived(act.at[pl.ds(at, QUART)], asem.at[2, d])


def body(tokens, gain_attn, w_query, query_bias, cache_keys, cache_values, w_out, gain_ffn, w_gate, w_up, w_down):
    v = pltpu.VMEM
    eight = (LINE, PK, 128)
    chunks = (8, LINE, PK, 128)
    sem = pltpu.SemaphoreType.DMA
    scratch = [
        v((TOK, D), BF), v((D // 128, 128), F32), v((COL, D), BF), v((1, COL), F32), v((CTX, HEAD), BF),
        v((CTX, HEAD), BF), v((COL, D), BF), v((1, COL), F32), v((HID, FEAT), BF), v((HID, FEAT), BF),
        v((HIDP, FEAT), BF),
        v((2 * TOK, D), BF),
        v((HEAD, CTX), BF),
        v((FEAT, HIDP), BF),
        v((COL, 128), F32),
        v((128, SEQ * PK), BF),
        v((FEAT, ALL), F32),
        v((FEAT + 8, ALL), F32),
        v((8, 8, ALL), F32),
        v(chunks, BF), v(chunks, BF),
        v(eight, BF), v(eight, BF), v(eight, BF),
        v(chunks, BF), v(chunks, BF), v(chunks, BF),
        v(chunks, BF), v(chunks, BF),
        v(eight, BF), v(eight, BF), v(eight, BF), v(eight, BF),
        v((2, HIDP, ALL), F32),
        v((MP, 2 * QUART + 16, ALL), BF), v((MP, 2 * QUART + 16, ALL), BF),
        v((HIDP, ALL), BF),
        v((PK, 128), F32),
        sem((11,)), sem((5,)), sem((5, LINE)), sem((5,)), sem((5,)), sem((5, LINE)), sem((4, MP)),
    ]
    any_space = pl.BlockSpec(memory_space=pl.ANY)
    attended, layer = pl.pallas_call(
        kernel,
        out_shape=(jax.ShapeDtypeStruct((COL, TOK), BF), jax.ShapeDtypeStruct((COL, TOK), BF)),
        in_specs=[any_space] * 11,
        out_specs=(pl.BlockSpec(memory_space=pltpu.VMEM), pl.BlockSpec(memory_space=pltpu.VMEM)),
        scratch_shapes=scratch,
        compiler_params=pltpu.CompilerParams(
            collective_id=0, has_side_effects=True, vmem_limit_bytes=66700000
        ),
        name="layer",
    )(
        tokens, gain_attn.reshape(D // 128, 128), w_query.T, query_bias.reshape(1, COL), cache_keys, cache_values,
        w_out.T, gain_ffn.reshape(1, COL), w_gate.T, w_up.T, w_down,
    )
    return attended.T, layer.T


def solution(mesh):
    placed = (
        P("mp", None), P(), P(None, "seq"), P("seq"), P(None, "seq", None), P(None, "seq", None),
        P(None, "seq"), P("seq"), P("mp", "seq"), P("mp", "seq"), P("seq", "mp"),
    )
    return jax.shard_map(
        body, mesh=mesh, in_specs=placed, out_specs=(P("mp", "seq"), P("mp", "seq")), check_vma=False
    )
```

time: 129 us -> 91.2 us (0.71)
  Pallas kernels: 117 us -> 88.5 us
  local copies, waits for them, and re-layouts: 10.5 us -> 1.92 us
    pallas_call x1, Pallas kernels: 117 us -> 88.5 us  [body(): pl.pallas_call(kernel, out_shape=(jax.ShapeDtypeStruct((COL, TOK), BF), j...]
    unnamed x22 -> x4, local copies, waits for them, and re-layouts: 9.8 us -> 1.92 us
where the time goes in v1:
time: 91.2 us; the launch traced here: 91 us
  Pallas kernels  88.5 us (97%)
  local copies, waits for them, and re-layouts  1.92 us (2%)
    pallas_call x1, Pallas kernels, body(): pl.pallas_call(kernel, out_shape=(jax.ShapeDtypeStruct((COL, TOK), BF), j...  88.5 us
    unnamed x4, local copies, waits for them, and re-layouts  1.92 us

profile of v1, /device:TPU:1, one launch (start us, length us, event | category | flops | bytes accessed | tf_op | source)
XLA Modules:
  0.0 91.0 jit_solution(7556615240539869368)
XLA Ops:
  0.6 88.5 %layer.1 = (bf16[56,64]{1,0:T(8,128)(2,1)}, bf16[56,64]{1,0:T(8,128)(2,1)}) custom-call(bf16[64,3584]{1,0:T(8,128)(2,1)} %tokens_h.1, f32[28,128]{1,0:T(8,128)} %bitcast.13, bf16[56,3584]{1,0:T(8,128)(2,1)} %bitcast.11, f32[1,56]{1,0:T(1,128)} %bitcast.16, bf16[4,1024,128]{2,1,0:T(8,128)(2,1)} %keys_h.1, bf16[4,1024,128]{2,1,0:T(8,128)(2,1)} %values_h.1, ...), custom_call_target="tpu_custom_call" | custom-call | tf_op jit(solution)/shard_map/layer/pallas_call | solution.py:465
  89.1 0.0 copy-start
  89.1 1.3 %copy.15 = bf16[64,56]{0,1:T(8,128)(2,1)} copy(bf16[64,56]{0,1:T(8,128)(2,1)} %bitcast.15) | data formatting | bytes 14336
  90.4 0.0 copy-done
  90.4 0.6 copy.16
Async XLA Ops:
  89.1 1.3 %copy-start = (bf16[56,64]{1,0:T(8,128)(2,1)S(1)}, bf16[56,64]{1,0:T(8,128)(2,1)}, u32[]{:S(2)}) copy-start(bf16[56,64]{1,0:T(8,128)(2,1)} %get-tuple-element.5) | copy-start | bytes 21508

commit v2 on v1

--- a/solution.py
+++ b/solution.py
@@ -67,11 +67,11 @@
     return jnp.where(at == 0, first, jnp.where(at == 1, second, jnp.where(at == 2, third, 0.0)))
 
 
-def merge_eight(chunks, j):
+def merge(chunks, j):
     at = row_ids(8)
-    high = jnp.logical_not(low_lanes(8))
+    high = jnp.logical_not(low_lanes(chunks.shape[0]))
     sides = ([], [])
-    for i in range(8):
+    for i in range(chunks.shape[0]):
         part = chunks[i, 24:PK]
         sides[0].append(jnp.sum(jnp.where(at < 3, part, 0.0), axis=0, keepdims=True))
         sides[1].append(jnp.sum(jnp.where(jnp.logical_and(at >= 3, at < 6), part, 0.0), axis=0, keepdims=True))
@@ -87,7 +87,7 @@
     edge = HEAD * ((j * COL) // HEAD + 1) - j * COL
     first_head = row_ids(PK) + jnp.where(low_lanes(PK), 0, PK) < edge
     acc = jnp.zeros((PK, 128), F32)
-    for i in range(8):
+    for i in range(chunks.shape[0]):
         acc += chunks[i] * jnp.where(first_head, weights[0][i : i + 1], weights[1][i : i + 1])
     return acc, levels
 
@@ -97,19 +97,20 @@
     att_out, lay_out,
     tokens, gain_attn, wq, bias, keys, values, wo, gain_ffn, wg, wu, wd,
     normed, value_t, wd_t, hid_t, wo_e, work, outs, lsplit, stage2, stage6,
-    line1, line3, line4, buf1, buf3, buf4, plane2, plane6, rel2, rel6, line2, line6,
+    own1, own4, held1, line3, held4, buf1, buf3, buf4, plane2, plane6, rel2, rel6, held2, held6,
     gu, gstage, gbuf, act, res,
     in_sem, zsend, zrecv, psend, precv, rrecv, asem,
 ):
     s = lax.axis_index("seq")
     m = lax.axis_index("mp")
-    own_m = s // PEER
-    own_j = lax.rem(s, PEER)
-    z = lax.rem(s, LINE)
+    z, x, yh = lax.rem(s, LINE), lax.rem(s // LINE, 4), s // (4 * LINE)
+    yl, c = m // 2, lax.rem(m, 2)
     line = s - z
     here = s // LINE
-    mine = own_m == m
-    group = (own_j // LINE) * MP + m
+    xb = lax.rem(x, 2)
+    own_j = LINE * xb + z
+    mine = x // 2 == c
+    same_y = yl == yh
 
     pairs = (
         (tokens_h, tokens), (gain_attn_h, gain_attn), (wq_h, wq), (bias_h, bias),
@@ -125,24 +126,14 @@
     def greet(p, q):
         pl.semaphore_signal(bar, inc=1, device_id=(p, q), device_id_type=MESH)
 
-    for d in range(1, LINE):
-        greet(line + lax.rem(z + d, LINE), m)
-    for g in range(8):
-        p, q = PEER * m + LINE * (g // MP) + z, g % MP
-        local = jnp.logical_and(p == s, q == m)
-
-        @pl.when(jnp.logical_not(local))
-        def _(p=p, q=q):
-            greet(p, q)
-
-        @pl.when(jnp.logical_not(jnp.logical_and(here == g, mine)))
-        def _(g=g):
-            greet(LINE * g + z, own_m)
-
-    for d in range(1, 8):
-        greet(LINE * lax.rem(here + d, 8) + z, m)
-    for d in range(1, MP):
-        greet(s, lax.rem(m + d, MP))
+    for i in range(1, 32):
+        u, v, d = i // 16, (i // 8) % 2, i % 8
+        greet(32 * lax.rem(yh + u, 2) + LINE * x + lax.rem(z + d, LINE), 2 * lax.rem(yl + v, 2) + c)
+    for i in range(1, 8):
+        greet(32 * yh + LINE * lax.rem(x + i % 4, 4) + z, 2 * yl + lax.rem(c + i // 4, 2))
+    for i in range(1, 4):
+        greet(32 * (1 - yh) + LINE * lax.rem(x + i, 4) + z, m)
+    greet(s, 2 * (1 - yl) + 1 - c)
 
     loads[0].wait()
     loads[1].wait()
@@ -166,64 +157,81 @@
         hi = jnp.concatenate([x[PK:COL], jnp.zeros((8, 128), F32)], axis=0)
         return jnp.where(low32, x[0:PK], swap(hi))
 
+    def remote(src, dst, send_sem, recv_sem, p, q):
+        pltpu.make_async_remote_copy(
+            src_ref=src, dst_ref=dst, send_sem=send_sem, recv_sem=recv_sem, device_id=(p, q), device_id_type=MESH
+        ).start()
+
+    def copy(src, dst, send_sem, recv_sem, p, q, local):
+        @pl.when(local)
+        def _():
+            pltpu.make_async_copy(src, dst, recv_sem).start()
+
+        @pl.when(jnp.logical_not(local))
+        def _():
+            remote(src, dst, send_sem, recv_sem, p, q)
+
+    def arrived(buf, sem):
+        pltpu.make_async_copy(buf, buf, sem).wait()
+
+    def near_first(i):
+        return lax.rem(jnp.where(lax.rem(i, 2) == 1, (i + 1) // 2, LINE - i // 2), LINE)
+
+    def far_first(i):
+        return lax.rem(LINE + LINE // 2 + jnp.where(lax.rem(i, 2) == 1, -((i + 1) // 2), i // 2), LINE)
+
+    def spread_yz(own, held, k):
+        for d in (4, 3, 5, 2, 6, 1, 7, 0):
+            for u in range(2):
+                to = (32 * u + LINE * x + lax.rem(z + d, LINE), 2 * yh + c)
+                sems = (zsend.at[k], zrecv.at[k, (LINE - d) % LINE])
+                slot = held.at[2 * z + yl]
+                if d:
+                    remote(own, slot, *sems, *to)
+                else:
+                    copy(own, slot, *sems, *to, jnp.logical_and(yh == u, same_y))
+
+    def spread_x(held, buf, k):
+        def step(i, carry):
+            e = near_first(i)
+            pair = pl.ds(2 * lax.rem(z + e, LINE), 2)
+            arrived(held.at[pair], zrecv.at[k, e])
+            for o in (2, 1, 3, 0):
+                to = (32 * yh + LINE * lax.rem(x + o, 4) + z, 2 * yl + x // 2)
+                args = (held.at[pair], buf.at[2 * xb + c, pair], psend.at[k], precv.at[k], *to)
+                if o:
+                    remote(*args)
+                else:
+                    copy(*args, mine)
+            return carry
+
+        lax.fori_loop(0, LINE, step, 0)
+
     def along_line(held, k):
         for d in (4, 3, 5, 2, 6, 1, 7):
-            pltpu.make_async_remote_copy(
-                src_ref=held.at[z], dst_ref=held.at[z], send_sem=zsend.at[k], recv_sem=zrecv.at[k, LINE - d],
-                device_id=(line + lax.rem(z + d, LINE), m), device_id_type=MESH,
-            ).start()
-
-    def on_to_plane(held, buf, k, target, place, own, first, last):
-        def step(i, c):
-            e = lax.rem(jnp.where(lax.rem(i, 2) == 1, (i + 1) // 2, LINE - i // 2), LINE)
+            remote(held.at[z], held.at[z], zsend.at[k], zrecv.at[k, LINE - d], line + lax.rem(z + d, LINE), m)
+
+    def on_to_plane(held, buf, k):
+        def step(i, carry):
+            e = near_first(i)
             at = lax.rem(z + e, LINE)
 
             @pl.when(i > 0)
             def _():
-                pltpu.make_async_copy(held.at[at], held.at[at], zrecv.at[k, e]).wait()
+                arrived(held.at[at], zrecv.at[k, e])
 
             for d in range(1, 8):
-                p = lax.rem(here + d, 8)
-                pltpu.make_async_remote_copy(
-                    src_ref=held.at[at], dst_ref=buf.at[place, at], send_sem=psend.at[k], recv_sem=precv.at[k],
-                    device_id=(LINE * p + z, target), device_id_type=MESH,
-                ).start()
-
-            @pl.when(own)
-            def _():
-                pltpu.make_async_copy(held.at[at], buf.at[place, at], precv.at[k]).start()
-
-            @pl.when(jnp.logical_not(own))
-            def _():
-                pltpu.make_async_remote_copy(
-                    src_ref=held.at[at], dst_ref=buf.at[place, at], send_sem=psend.at[k], recv_sem=precv.at[k],
-                    device_id=(s, target), device_id_type=MESH,
-                ).start()
-
-            return c
-
-        lax.fori_loop(first, last, step, 0)
-
-    def arrived(buf, sem):
-        pltpu.make_async_copy(buf, buf, sem).wait()
-
-    def sent(buf, sem, own):
-        @pl.when(own)
-        def _():
-            arrived(buf.at[pl.ds(0, 7)], sem)
-
-        @pl.when(jnp.logical_not(own))
-        def _():
-            arrived(buf, sem)
-
-    line1[z] = packed(q_t).astype(BF)
-    pl.semaphore_wait(bar, 7 + jnp.where(mine, 14, 16) + 7 + MP - 1)
-    along_line(line1, 0)
-    on_to_plane(line1, buf1, 0, own_m, group, mine, 0, 1)
+                p = LINE * lax.rem(here + d, 8) + z
+                remote(held.at[at], buf.at[here, at], psend.at[k], precv.at[k], p, m)
+            pltpu.make_async_copy(held.at[at], buf.at[here, at], precv.at[k]).start()
+            return carry
+
+        lax.fori_loop(0, LINE, step, 0)
+
+    own1[...] = packed(q_t).astype(BF)
 
     loads[5].wait()
     value_t[...] = values[...].T
-    on_to_plane(line1, buf1, 0, own_m, group, mine, 1, LINE)
     first = lax.broadcasted_iota(jnp.int32, (COL, D), 1) - lax.broadcasted_iota(jnp.int32, (COL, D), 0)
     pick = jnp.where(first == s * COL, 1.0, 0.0).astype(BF)
     normed[pl.ds(0, TOK), :] = tokens[...]
@@ -248,12 +256,16 @@
     for i in (4, 7, 8, 9):
         loads[i].wait()
 
+    pl.semaphore_wait(bar, 42)
+    spread_yz(own1, held1, 0)
+    spread_x(held1, buf1, 0)
+
     def unpack_chunks(buf, squares):
         def one(j, sums):
             sums = list(sums)
             for t in range(2):
-                a = buf[(j // LINE) * MP + 2 * t, lax.rem(j, LINE)].astype(F32)
-                b = buf[(j // LINE) * MP + 2 * t + 1, lax.rem(j, LINE)].astype(F32)
+                a = buf[2 * (j // LINE), 2 * lax.rem(j, LINE) + t].astype(F32)
+                b = buf[2 * (j // LINE) + 1, 2 * lax.rem(j, LINE) + t].astype(F32)
                 lo = jnp.where(low32, a, swap(b))
                 hi = jnp.where(low32, swap(a), b)
                 at = pl.multiple_of(j * COL, 8)
@@ -268,11 +280,8 @@
 
     low8 = low_lanes(8)
 
-    def far_first(i):
-        return lax.rem(LINE + LINE // 2 + jnp.where(lax.rem(i, 2) == 1, -((i + 1) // 2), i // 2), LINE)
-
-    def to_plane(stage, plane, k, stats):
-        def step(i, c):
+    def collect_x(stage, plane, k, stats):
+        def step(i, carry):
             e = far_first(i)
             to_z = lax.rem(z + e, LINE)
             for half in range(2):
@@ -290,43 +299,30 @@
                         )
                         a = jnp.concatenate([a[0:24], jnp.where(low8, a[24:PK], swap(both))], axis=0)
                         b = jnp.concatenate([b[0:24], jnp.where(low8, b[24:PK], both)], axis=0)
-                    stage[to_z, half * MP + 2 * t] = a.astype(BF)
-                    stage[to_z, half * MP + 2 * t + 1] = b.astype(BF)
-            for g in range(8):
-                p, q = PEER * m + LINE * (g // MP) + z, g % MP
-                local = jnp.logical_and(p == s, q == m)
-
-                @pl.when(local)
-                def _():
-                    pltpu.make_async_copy(stage.at[to_z, g], plane.at[to_z, here], rrecv.at[k, e]).start()
-
-                @pl.when(jnp.logical_not(local))
-                def _():
-                    pltpu.make_async_remote_copy(
-                        src_ref=stage.at[to_z, g], dst_ref=plane.at[to_z, here],
-                        send_sem=psend.at[k], recv_sem=rrecv.at[k, e], device_id=(p, q), device_id_type=MESH,
-                    ).start()
-
-            return c
+                    stage[to_z, 2 * half, t] = a.astype(BF)
+                    stage[to_z, 2 * half + 1, t] = b.astype(BF)
+            for g in range(4):
+                to = (32 * yh + LINE * (2 * c + g // 2) + z, 2 * yl + g % 2)
+                local = jnp.logical_and(2 * c + g // 2 == x, g % 2 == c)
+                copy(stage.at[to_z, g], plane.at[to_z, x], psend.at[k], rrecv.at[k, e], *to, local)
+            return carry
 
         lax.fori_loop(0, LINE, step, 0)
 
-    def pass_on(plane, rel, held, k, join):
-        def step(i, c):
+    def collect_yz(plane, rel, held, k, join):
+        def step(i, carry):
             e = far_first(i)
             to_z = lax.rem(z + e, LINE)
             arrived(plane.at[to_z], rrecv.at[k, e])
-            rel[to_z] = join(plane[to_z].astype(F32), to_z).astype(BF)
-            pltpu.make_async_remote_copy(
-                src_ref=rel.at[to_z], dst_ref=held.at[z], send_sem=zsend.at[k], recv_sem=zrecv.at[k, 0],
-                device_id=(line + to_z, m), device_id_type=MESH,
-            ).start()
-            return c
-
-        lax.fori_loop(0, LINE - 1, step, 0)
-        arrived(plane.at[z], rrecv.at[k, 0])
-        held[z] = join(plane[z].astype(F32), z).astype(BF)
-        arrived(held.at[pl.ds(0, 7)], zrecv.at[k, 0])
+            for t in range(2):
+                rel[2 * to_z + t] = join(plane[to_z, :, t].astype(F32), to_z).astype(BF)
+                local = jnp.logical_and(jnp.logical_and(same_y, e == 0), yl == t)
+                to = (32 * yl + LINE * x + to_z, 2 * t + c)
+                copy(rel.at[2 * to_z + t], held.at[2 * z + yh], zsend.at[k], zrecv.at[k, 0], *to, local)
+            return carry
+
+        lax.fori_loop(0, LINE, step, 0)
+        arrived(held, zrecv.at[k, 0])
 
     arrived(buf1, precv.at[0])
     unpack_chunks(buf1, False)
@@ -345,19 +341,19 @@
 
     lax.fori_loop(0, GROUP, one_head, 0)
 
-    to_plane(stage2, plane2, 1, True)
+    collect_x(stage2, plane2, 1, True)
 
     def join2(chunks, to_z):
-        value, levels = merge_eight(chunks, (own_j // LINE) * LINE + to_z)
+        value, levels = merge(chunks, LINE * xb + to_z)
         rows = three_rows(levels[0], 8) + three_rows(levels[1], 8, 3)
         return jnp.concatenate([value[0:24], jnp.where(low8, value[24:PK], rows)], axis=0)
 
-    pass_on(plane2, rel2, line2, 1, join2)
-    merged = merge_eight(line2[...].astype(F32), own_j)[0].astype(BF)
+    collect_yz(plane2, rel2, held2, 1, join2)
+    merged = merge(held2[...].astype(F32), own_j)[0].astype(BF)
     line3[z] = merged
 
     along_line(line3, 2)
-    on_to_plane(line3, buf3, 2, m, here, True, 0, LINE)
+    on_to_plane(line3, buf3, 2)
 
     def unpacked(x, out):
         out[pl.ds(0, PK), :] = x[:, 0:64].astype(BF)
@@ -376,9 +372,9 @@
     squares = jnp.sum(jnp.where(real, residual * residual, 0.0), axis=0, keepdims=True)
     squares = squares + swap(squares)
     scaled = residual * gain_pk
-    line4[z] = jnp.where(real, scaled, three_rows(squares, PK, 24)).astype(BF)
-    along_line(line4, 3)
-    on_to_plane(line4, buf4, 3, own_m, group, mine, 0, LINE)
+    own4[...] = jnp.where(real, scaled, three_rows(squares, PK, 24)).astype(BF)
+    spread_yz(own4, held4, 3)
+    spread_x(held4, buf4, 3)
     arrived(buf4, precv.at[3])
     sums = unpack_chunks(buf4, True)
     sq = jnp.concatenate([jnp.sum(x, axis=0, keepdims=True) for x in sums], axis=1)
@@ -419,14 +415,26 @@
         arrived(act.at[pl.ds(pl.multiple_of(lax.rem(m + MP - d, MP) * QUART, 16), QUART)], asem.at[3, d])
 
     outs[pl.ds(0, FEAT), :] = dot(wd_t[...], act[...])
-    to_plane(stage6, plane6, 4, False)
-    pass_on(plane6, rel6, line6, 4, lambda chunks, to_z: jnp.sum(chunks, axis=0))
-    unpacked(res[...] + jnp.sum(line6[...].astype(F32), axis=0), lay_out)
-
-    for k in range(5):
-        arrived(line1.at[pl.ds(0, 7)], zsend.at[k])
-    for k, buf in ((0, buf1), (1, plane2), (3, buf4), (4, plane6)):
-        sent(buf, psend.at[k], mine)
+    collect_x(stage6, plane6, 4, False)
+    collect_yz(plane6, rel6, held6, 4, lambda chunks, to_z: jnp.sum(chunks, axis=0))
+    unpacked(res[...] + jnp.sum(held6[...].astype(F32), axis=0), lay_out)
+
+    for k, buf in ((0, buf1), (1, stage2), (3, buf4), (4, stage6)):
+        for own, some, sem in ((same_y, held1.at[pl.ds(0, 15)], zsend.at[k]), (mine, None, psend.at[k])):
+            whole = held1 if some is not None else buf
+            part = some
+            if part is None:
+                part = buf.at[pl.ds(0, 3)] if buf.shape[0] == 4 else buf.at[pl.ds(0, 6)]
+
+            @pl.when(own)
+            def _(part=part, sem=sem):
+                arrived(part, sem)
+
+            @pl.when(jnp.logical_not(own))
+            def _(whole=whole, sem=sem):
+                arrived(whole, sem)
+
+    arrived(line3.at[pl.ds(0, 7)], zsend.at[2])
     arrived(buf3.at[pl.ds(0, 7)], psend.at[2])
     for d in range(1, MP):
         arrived(gstage.at[d], asem.at[0, d])
@@ -435,8 +443,8 @@
 
 def body(tokens, gain_attn, w_query, query_bias, cache_keys, cache_values, w_out, gain_ffn, w_gate, w_up, w_down):
     v = pltpu.VMEM
-    eight = (LINE, PK, 128)
-    chunks = (8, LINE, PK, 128)
+    one, eight, pairs = (PK, 128), (LINE, PK, 128), (2 * LINE, PK, 128)
+    chunks, users, owners = (8, LINE, PK, 128), (4, 2 * LINE, PK, 128), (LINE, 4, 2, PK, 128)
     sem = pltpu.SemaphoreType.DMA
     scratch = [
         v((TOK, D), BF), v((D // 128, 128), F32), v((COL, D), BF), v((1, COL), F32), v((CTX, HEAD), BF),
@@ -450,11 +458,11 @@
         v((FEAT, ALL), F32),
         v((FEAT + 8, ALL), F32),
         v((8, 8, ALL), F32),
-        v(chunks, BF), v(chunks, BF),
-        v(eight, BF), v(eight, BF), v(eight, BF),
-        v(chunks, BF), v(chunks, BF), v(chunks, BF),
-        v(chunks, BF), v(chunks, BF),
-        v(eight, BF), v(eight, BF), v(eight, BF), v(eight, BF),
+        v(owners, BF), v(owners, BF),
+        v(one, BF), v(one, BF), v(pairs, BF), v(eight, BF), v(pairs, BF),
+        v(users, BF), v(chunks, BF), v(users, BF),
+        v(owners, BF), v(owners, BF),
+        v(pairs, BF), v(pairs, BF), v(pairs, BF), v(pairs, BF),
         v((2, HIDP, ALL), F32),
         v((MP, 2 * QUART + 16, ALL), BF), v((MP, 2 * QUART + 16, ALL), BF),
         v((HIDP, ALL), BF),

time: 91.2 us -> 89.7 us (0.984)
  Pallas kernels: 88.5 us -> 87 us
    pallas_call x1, Pallas kernels: 88.5 us -> 87 us  [body(): pl.pallas_call(kernel, out_shape=(jax.ShapeDtypeStruct((COL, TOK), BF), j...]
where the time goes in v2:
time: 89.7 us; the launch traced here: 89.5 us
  Pallas kernels  87 us (97%)
  local copies, waits for them, and re-layouts  1.92 us (2%)
    pallas_call x1, Pallas kernels, body(): pl.pallas_call(kernel, out_shape=(jax.ShapeDtypeStruct((COL, TOK), BF), j...  87 us
    unnamed x4, local copies, waits for them, and re-layouts  1.92 us

profile of v2, /device:TPU:1, one launch (start us, length us, event | category | flops | bytes accessed | tf_op | source)
XLA Modules:
  0.0 89.5 jit_solution(9924337367993710825)
XLA Ops:
  0.6 87.0 %layer.1 = (bf16[56,64]{1,0:T(8,128)(2,1)}, bf16[56,64]{1,0:T(8,128)(2,1)}) custom-call(bf16[64,3584]{1,0:T(8,128)(2,1)} %tokens_h.1, f32[28,128]{1,0:T(8,128)} %bitcast.13, bf16[56,3584]{1,0:T(8,128)(2,1)} %bitcast.11, f32[1,56]{1,0:T(1,128)} %bitcast.16, bf16[4,1024,128]{2,1,0:T(8,128)(2,1)} %keys_h.1, bf16[4,1024,128]{2,1,0:T(8,128)(2,1)} %values_h.1, ...), custom_call_target="tpu_custom_call" | custom-call | tf_op jit(solution)/shard_map/layer/pallas_call | solution.py:473
  87.6 0.0 copy-start
  87.6 1.3 %copy.15 = bf16[64,56]{0,1:T(8,128)(2,1)} copy(bf16[64,56]{0,1:T(8,128)(2,1)} %bitcast.15) | data formatting | bytes 14336
  88.9 0.0 copy-done
  88.9 0.6 copy.16
Async XLA Ops:
  87.6 1.3 %copy-start = (bf16[56,64]{1,0:T(8,128)(2,1)S(1)}, bf16[56,64]{1,0:T(8,128)(2,1)}, u32[]{:S(2)}) copy-start(bf16[56,64]{1,0:T(8,128)(2,1)} %get-tuple-element.5) | copy-start | bytes 21508

commit v3 on v2

--- a/solution.py
+++ b/solution.py
@@ -184,32 +184,34 @@
         for d in (4, 3, 5, 2, 6, 1, 7, 0):
             for u in range(2):
                 to = (32 * u + LINE * x + lax.rem(z + d, LINE), 2 * yh + c)
-                sems = (zsend.at[k], zrecv.at[k, (LINE - d) % LINE])
-                slot = held.at[2 * z + yl]
+                sems = (zsend.at[k], zrecv.at[k, yl, (LINE - d) % LINE])
+                slot = held.at[yl, z]
                 if d:
                     remote(own, slot, *sems, *to)
                 else:
                     copy(own, slot, *sems, *to, jnp.logical_and(yh == u, same_y))
 
     def spread_x(held, buf, k):
-        def step(i, carry):
-            e = near_first(i)
-            pair = pl.ds(2 * lax.rem(z + e, LINE), 2)
-            arrived(held.at[pair], zrecv.at[k, e])
-            for o in (2, 1, 3, 0):
-                to = (32 * yh + LINE * lax.rem(x + o, 4) + z, 2 * yl + x // 2)
-                args = (held.at[pair], buf.at[2 * xb + c, pair], psend.at[k], precv.at[k], *to)
-                if o:
-                    remote(*args)
-                else:
-                    copy(*args, mine)
-            return carry
-
-        lax.fori_loop(0, LINE, step, 0)
+        for t in range(2):
+
+            def step(i, carry, t=t):
+                e = near_first(i)
+                at = lax.rem(z + e, LINE)
+                arrived(held.at[t, at], zrecv.at[k, t, e])
+                for o in (2, 1, 3, 0):
+                    to = (32 * yh + LINE * lax.rem(x + o, 4) + z, 2 * yl + x // 2)
+                    args = (held.at[t, at], buf.at[t, 2 * xb + c, at], psend.at[k], precv.at[k, t], *to)
+                    if o:
+                        remote(*args)
+                    else:
+                        copy(*args, mine)
+                return carry
+
+            lax.fori_loop(0, LINE, step, 0)
 
     def along_line(held, k):
         for d in (4, 3, 5, 2, 6, 1, 7):
-            remote(held.at[z], held.at[z], zsend.at[k], zrecv.at[k, LINE - d], line + lax.rem(z + d, LINE), m)
+            remote(held.at[z], held.at[z], zsend.at[k], zrecv.at[k, 0, LINE - d], line + lax.rem(z + d, LINE), m)
 
     def on_to_plane(held, buf, k):
         def step(i, carry):
@@ -218,12 +220,12 @@
 
             @pl.when(i > 0)
             def _():
-                arrived(held.at[at], zrecv.at[k, e])
+                arrived(held.at[at], zrecv.at[k, 0, e])
 
             for d in range(1, 8):
                 p = LINE * lax.rem(here + d, 8) + z
-                remote(held.at[at], buf.at[here, at], psend.at[k], precv.at[k], p, m)
-            pltpu.make_async_copy(held.at[at], buf.at[here, at], precv.at[k]).start()
+                remote(held.at[at], buf.at[here, at], psend.at[k], precv.at[k, 0], p, m)
+            pltpu.make_async_copy(held.at[at], buf.at[here, at], precv.at[k, 0]).start()
             return carry
 
         lax.fori_loop(0, LINE, step, 0)
@@ -260,88 +262,94 @@
     spread_yz(own1, held1, 0)
     spread_x(held1, buf1, 0)
 
-    def unpack_chunks(buf, squares):
-        def one(j, sums):
-            sums = list(sums)
-            for t in range(2):
-                a = buf[2 * (j // LINE), 2 * lax.rem(j, LINE) + t].astype(F32)
-                b = buf[2 * (j // LINE) + 1, 2 * lax.rem(j, LINE) + t].astype(F32)
-                lo = jnp.where(low32, a, swap(b))
-                hi = jnp.where(low32, swap(a), b)
-                at = pl.multiple_of(j * COL, 8)
-                work[pl.ds(at, PK), pl.ds(128 * t, 128)] = lo
-                work[pl.ds(pl.multiple_of(at + PK, 8), COL - PK), pl.ds(128 * t, 128)] = hi[0 : COL - PK]
-                if squares:
-                    sums[t] = sums[t] + hi[COL - PK : PK]
-            return tuple(sums)
-
-        zero = jnp.zeros((8, 128), F32)
-        return lax.fori_loop(0, PEER, one, (zero, zero), unroll=4)
+    def unpack_chunks(buf, t, squares):
+        tile = pl.ds(128 * t, 128)
+
+        def one(j, total):
+            a = buf[t, 2 * (j // LINE), lax.rem(j, LINE)].astype(F32)
+            b = buf[t, 2 * (j // LINE) + 1, lax.rem(j, LINE)].astype(F32)
+            lo = jnp.where(low32, a, swap(b))
+            hi = jnp.where(low32, swap(a), b)
+            at = pl.multiple_of(j * COL, 8)
+            work[pl.ds(at, PK), tile] = lo
+            work[pl.ds(pl.multiple_of(at + PK, 8), COL - PK), tile] = hi[0 : COL - PK]
+            return total + hi[COL - PK : PK] if squares else total
+
+        return lax.fori_loop(0, PEER, one, jnp.zeros((8, 128), F32), unroll=4)
 
     low8 = low_lanes(8)
 
-    def collect_x(stage, plane, k, stats):
+    def collect_x(stage, plane, k, t, stats):
+        tile = pl.ds(128 * t, 128)
+
         def step(i, carry):
             e = far_first(i)
             to_z = lax.rem(z + e, LINE)
             for half in range(2):
                 j = half * LINE + to_z
-                at = pl.multiple_of(j * COL, 8)
-                for t in range(2):
-                    r = outs[pl.ds(at, 2 * PK), pl.ds(128 * t, 128)]
-                    lo, hi = r[0:PK], r[PK : 2 * PK]
-                    a = jnp.where(low32, lo, swap(hi))
-                    b = jnp.where(low32, swap(lo), hi)
-                    if stats:
-                        h0, h1 = (j * COL) // HEAD, (j * COL + COL - 1) // HEAD
-                        both = jnp.where(
-                            row_ids(8) < 3, lsplit[h0, :, pl.ds(128 * t, 128)], lsplit[h1, :, pl.ds(128 * t, 128)]
-                        )
-                        a = jnp.concatenate([a[0:24], jnp.where(low8, a[24:PK], swap(both))], axis=0)
-                        b = jnp.concatenate([b[0:24], jnp.where(low8, b[24:PK], both)], axis=0)
-                    stage[to_z, 2 * half, t] = a.astype(BF)
-                    stage[to_z, 2 * half + 1, t] = b.astype(BF)
+                r = outs[pl.ds(pl.multiple_of(j * COL, 8), 2 * PK), tile]
+                lo, hi = r[0:PK], r[PK : 2 * PK]
+                a = jnp.where(low32, lo, swap(hi))
+                b = jnp.where(low32, swap(lo), hi)
+                if stats:
+                    h0, h1 = (j * COL) // HEAD, (j * COL + COL - 1) // HEAD
+                    both = jnp.where(row_ids(8) < 3, lsplit[h0, :, tile], lsplit[h1, :, tile])
+                    a = jnp.concatenate([a[0:24], jnp.where(low8, a[24:PK], swap(both))], axis=0)
+                    b = jnp.concatenate([b[0:24], jnp.where(low8, b[24:PK], both)], axis=0)
+                stage[t, to_z, 2 * half] = a.astype(BF)
+                stage[t, to_z, 2 * half + 1] = b.astype(BF)
             for g in range(4):
                 to = (32 * yh + LINE * (2 * c + g // 2) + z, 2 * yl + g % 2)
                 local = jnp.logical_and(2 * c + g // 2 == x, g % 2 == c)
-                copy(stage.at[to_z, g], plane.at[to_z, x], psend.at[k], rrecv.at[k, e], *to, local)
+                copy(stage.at[t, to_z, g], plane.at[t, to_z, x], psend.at[k], rrecv.at[k, t, e], *to, local)
             return carry
 
         lax.fori_loop(0, LINE, step, 0)
 
     def collect_yz(plane, rel, held, k, join):
-        def step(i, carry):
-            e = far_first(i)
-            to_z = lax.rem(z + e, LINE)
-            arrived(plane.at[to_z], rrecv.at[k, e])
-            for t in range(2):
-                rel[2 * to_z + t] = join(plane[to_z, :, t].astype(F32), to_z).astype(BF)
+        for t in range(2):
+
+            def step(i, carry, t=t):
+                e = far_first(i)
+                to_z = lax.rem(z + e, LINE)
+                arrived(plane.at[t, to_z], rrecv.at[k, t, e])
+                rel[t, to_z] = join(plane[t, to_z].astype(F32), to_z).astype(BF)
                 local = jnp.logical_and(jnp.logical_and(same_y, e == 0), yl == t)
                 to = (32 * yl + LINE * x + to_z, 2 * t + c)
-                copy(rel.at[2 * to_z + t], held.at[2 * z + yh], zsend.at[k], zrecv.at[k, 0], *to, local)
-            return carry
-
-        lax.fori_loop(0, LINE, step, 0)
-        arrived(held, zrecv.at[k, 0])
-
-    arrived(buf1, precv.at[0])
-    unpack_chunks(buf1, False)
+                copy(rel.at[t, to_z], held.at[2 * z + yh], zsend.at[k], zrecv.at[k, 0, 0], *to, local)
+                return carry
+
+            lax.fori_loop(0, LINE, step, 0)
+        arrived(held, zrecv.at[k, 0, 0])
+
     scale = HEAD ** (-0.5) * LOG2E
 
-    def one_head(h, c):
-        at = pl.multiple_of(h * HEAD, HEAD)
-        scores = dot(keys[...], work[pl.ds(at, HEAD), :].astype(BF)) * scale
+    def attend(t, h, n):
+        tile = pl.ds(128 * t, 128)
+        rows = [pl.ds(pl.multiple_of((h + i) * HEAD, HEAD), HEAD) for i in range(n)]
+        queries = jnp.concatenate([work[r, tile].astype(BF) for r in rows], axis=1)
+        scores = dot(keys[...], queries) * scale
         top = jnp.max(scores, axis=0, keepdims=True)
         probs = jnp.exp2(scores - top)
         total = jnp.sum(probs, axis=0, keepdims=True)
-        outs[pl.ds(at, HEAD), :] = dot(value_t[...], probs.astype(BF)) * (1.0 / total)
+        value = dot(value_t[...], probs.astype(BF)) * (1.0 / total)
         level = top + jnp.log(total) * LOG2E
-        lsplit[h] = three_rows(level, 8) + three_rows(level, 8, 3)
-        return c
-
-    lax.fori_loop(0, GROUP, one_head, 0)
-
-    collect_x(stage2, plane2, 1, True)
+        parts = three_rows(level, 8) + three_rows(level, 8, 3)
+        for i in range(n):
+            outs[rows[i], tile] = value[:, 128 * i : 128 * (i + 1)]
+            lsplit[h + i, :, tile] = parts[:, 128 * i : 128 * (i + 1)]
+
+    for t in range(2):
+        arrived(buf1.at[t], precv.at[0, t])
+        unpack_chunks(buf1, t, False)
+
+        def two_heads(i, carry, t=t):
+            attend(t, 2 * i, 2)
+            return carry
+
+        lax.fori_loop(0, GROUP // 2, two_heads, 0)
+        attend(t, GROUP - 1, 1)
+        collect_x(stage2, plane2, 1, t, True)
 
     def join2(chunks, to_z):
         value, levels = merge(chunks, LINE * xb + to_z)
@@ -363,7 +371,7 @@
     res_hid = packed(hid_t[...])
     gain_col = jnp.broadcast_to(column_of(gain_ffn[...]), (COL, 128))
     gain_pk = packed(gain_col)
-    arrived(buf3, precv.at[2])
+    arrived(buf3, precv.at[2, 0])
     both = dot(wo_e[...], buf3[...].reshape(SEQ * PK, 128))
     residual = res_hid + packed(both[0:COL] + swap(both[64 : 64 + COL]))
     res[...] = residual
@@ -375,56 +383,54 @@
     own4[...] = jnp.where(real, scaled, three_rows(squares, PK, 24)).astype(BF)
     spread_yz(own4, held4, 3)
     spread_x(held4, buf4, 3)
-    arrived(buf4, precv.at[3])
-    sums = unpack_chunks(buf4, True)
-    sq = jnp.concatenate([jnp.sum(x, axis=0, keepdims=True) for x in sums], axis=1)
-
-    features = work[pl.ds(0, FEAT), :].astype(BF)
-    gu[0, pl.ds(0, HID), :] = dot(wg[...], features)
-    gu[1, pl.ds(0, HID), :] = dot(wu[...], features)
-    sq_rows = three_rows(sq, 16).astype(BF)
-    for d in range(1, MP):
-        q = lax.rem(m + d, MP)
-        at = pl.multiple_of(q * QUART, 16)
-        gstage[d, pl.ds(0, QUART), :] = gu[0, pl.ds(at, QUART), :].astype(BF)
-        gstage[d, pl.ds(QUART, QUART), :] = gu[1, pl.ds(at, QUART), :].astype(BF)
-        gstage[d, pl.ds(2 * QUART, 16), :] = sq_rows
-        pltpu.make_async_remote_copy(
-            src_ref=gstage.at[d], dst_ref=gbuf.at[d], send_sem=asem.at[0, d], recv_sem=asem.at[1, d],
-            device_id=(s, q), device_id_type=MESH,
-        ).start()
+
+    sqs = []
+    for t in range(2):
+        tile = pl.ds(128 * t, 128)
+        arrived(buf4.at[t], precv.at[3, t])
+        sq = jnp.sum(unpack_chunks(buf4, t, True), axis=0, keepdims=True)
+        features = work[pl.ds(0, FEAT), tile].astype(BF)
+        gu[0, pl.ds(0, HID), tile] = dot(wg[...], features)
+        gu[1, pl.ds(0, HID), tile] = dot(wu[...], features)
+        sq_rows = three_rows(sq, 16).astype(BF)
+        for d in (2, 3, 1):
+            q = lax.rem(m + d, MP)
+            at = pl.multiple_of(q * QUART, 16)
+            gstage[t, d, pl.ds(0, QUART)] = gu[0, pl.ds(at, QUART), tile].astype(BF)
+            gstage[t, d, pl.ds(QUART, QUART)] = gu[1, pl.ds(at, QUART), tile].astype(BF)
+            gstage[t, d, pl.ds(2 * QUART, 16)] = sq_rows
+            remote(gstage.at[t, d], gbuf.at[t, d], asem.at[0, t, d], asem.at[1, t, d], s, q)
+        sqs.append(sq)
     at = pl.multiple_of(m * QUART, 16)
-    gate = gu[0, pl.ds(at, QUART), :]
-    up = gu[1, pl.ds(at, QUART), :]
-    for d in range(1, MP):
-        arrived(gbuf.at[d], asem.at[1, d])
-        gate += gbuf[d, pl.ds(0, QUART), :].astype(F32)
-        up += gbuf[d, pl.ds(QUART, QUART), :].astype(F32)
-        sq += jnp.sum(gbuf[d, pl.ds(2 * QUART, 16), :].astype(F32), axis=0, keepdims=True)
-    factor = lax.rsqrt(sq * (1.0 / D) + EPS)
-    gate = gate * factor
-    up = up * factor
-    act[pl.ds(at, QUART), :] = (gate / (1.0 + jnp.exp(-gate)) * up).astype(BF)
-    for d in range(1, MP):
-        q = lax.rem(m + d, MP)
-        pltpu.make_async_remote_copy(
-            src_ref=act.at[pl.ds(at, QUART)], dst_ref=act.at[pl.ds(at, QUART)],
-            send_sem=asem.at[2, d], recv_sem=asem.at[3, d], device_id=(s, q), device_id_type=MESH,
-        ).start()
-    for d in range(1, MP):
-        arrived(act.at[pl.ds(pl.multiple_of(lax.rem(m + MP - d, MP) * QUART, 16), QUART)], asem.at[3, d])
-
-    outs[pl.ds(0, FEAT), :] = dot(wd_t[...], act[...])
-    collect_x(stage6, plane6, 4, False)
+    own_rows = pl.ds(at, QUART)
+    for t in range(2):
+        tile = pl.ds(128 * t, 128)
+        gate, up, sq = gu[0, own_rows, tile], gu[1, own_rows, tile], sqs[t]
+        for d in (1, 3, 2):
+            arrived(gbuf.at[t, d], asem.at[1, t, d])
+            gate += gbuf[t, d, pl.ds(0, QUART)].astype(F32)
+            up += gbuf[t, d, pl.ds(QUART, QUART)].astype(F32)
+            sq += jnp.sum(gbuf[t, d, pl.ds(2 * QUART, 16)].astype(F32), axis=0, keepdims=True)
+        factor = lax.rsqrt(sq * (1.0 / D) + EPS)
+        gate = gate * factor
+        up = up * factor
+        act[t, own_rows] = (gate / (1.0 + jnp.exp(-gate)) * up).astype(BF)
+        for d in (2, 3, 1):
+            part = act.at[t, own_rows]
+            remote(part, part, asem.at[2, t, d], asem.at[3, t, d], s, lax.rem(m + d, MP))
+
+    for t in range(2):
+        for d in (1, 3, 2):
+            rows = pl.ds(pl.multiple_of(lax.rem(m + MP - d, MP) * QUART, 16), QUART)
+            arrived(act.at[t, rows], asem.at[3, t, d])
+        outs[pl.ds(0, FEAT), pl.ds(128 * t, 128)] = dot(wd_t[...], act[t])
+        collect_x(stage6, plane6, 4, t, False)
     collect_yz(plane6, rel6, held6, 4, lambda chunks, to_z: jnp.sum(chunks, axis=0))
     unpacked(res[...] + jnp.sum(held6[...].astype(F32), axis=0), lay_out)
 
-    for k, buf in ((0, buf1), (1, stage2), (3, buf4), (4, stage6)):
-        for own, some, sem in ((same_y, held1.at[pl.ds(0, 15)], zsend.at[k]), (mine, None, psend.at[k])):
-            whole = held1 if some is not None else buf
-            part = some
-            if part is None:
-                part = buf.at[pl.ds(0, 3)] if buf.shape[0] == 4 else buf.at[pl.ds(0, 6)]
+    fifteen, most = held2.at[pl.ds(0, 15)], buf3.at[pl.ds(0, 6)]
+    for k in (0, 1, 3, 4):
+        for own, part, whole, sem in ((same_y, fifteen, held2, zsend.at[k]), (mine, most, buf3, psend.at[k])):
 
             @pl.when(own)
             def _(part=part, sem=sem):
@@ -436,15 +442,16 @@
 
     arrived(line3.at[pl.ds(0, 7)], zsend.at[2])
     arrived(buf3.at[pl.ds(0, 7)], psend.at[2])
-    for d in range(1, MP):
-        arrived(gstage.at[d], asem.at[0, d])
-        arrived(act.at[pl.ds(at, QUART)], asem.at[2, d])
+    for t in range(2):
+        for d in range(1, MP):
+            arrived(gstage.at[t, d], asem.at[0, t, d])
+            arrived(act.at[t, own_rows], asem.at[2, t, d])
 
 
 def body(tokens, gain_attn, w_query, query_bias, cache_keys, cache_values, w_out, gain_ffn, w_gate, w_up, w_down):
     v = pltpu.VMEM
-    one, eight, pairs = (PK, 128), (LINE, PK, 128), (2 * LINE, PK, 128)
-    chunks, users, owners = (8, LINE, PK, 128), (4, 2 * LINE, PK, 128), (LINE, 4, 2, PK, 128)
+    one, eight, pairs, halves = (PK, 128), (LINE, PK, 128), (2 * LINE, PK, 128), (2, LINE, PK, 128)
+    chunks, users, owners = (8, LINE, PK, 128), (2, 4, LINE, PK, 128), (2, LINE, 4, PK, 128)
     sem = pltpu.SemaphoreType.DMA
     scratch = [
         v((TOK, D), BF), v((D // 128, 128), F32), v((COL, D), BF), v((1, COL), F32), v((CTX, HEAD), BF),
@@ -459,15 +466,15 @@
         v((FEAT + 8, ALL), F32),
         v((8, 8, ALL), F32),
         v(owners, BF), v(owners, BF),
-        v(one, BF), v(one, BF), v(pairs, BF), v(eight, BF), v(pairs, BF),
+        v(one, BF), v(one, BF), v(halves, BF), v(eight, BF), v(halves, BF),
         v(users, BF), v(chunks, BF), v(users, BF),
         v(owners, BF), v(owners, BF),
-        v(pairs, BF), v(pairs, BF), v(pairs, BF), v(pairs, BF),
+        v(halves, BF), v(halves, BF), v(pairs, BF), v(pairs, BF),
         v((2, HIDP, ALL), F32),
-        v((MP, 2 * QUART + 16, ALL), BF), v((MP, 2 * QUART + 16, ALL), BF),
-        v((HIDP, ALL), BF),
+        v((2, MP, 2 * QUART + 16, 128), BF), v((2, MP, 2 * QUART + 16, 128), BF),
+        v((2, HIDP, 128), BF),
         v((PK, 128), F32),
-        sem((11,)), sem((5,)), sem((5, LINE)), sem((5,)), sem((5,)), sem((5, LINE)), sem((4, MP)),
+        sem((11,)), sem((5,)), sem((5, 2, LINE)), sem((5,)), sem((5, 2)), sem((5, 2, LINE)), sem((4, 2, MP)),
     ]
     any_space = pl.BlockSpec(memory_space=pl.ANY)
     attended, layer = pl.pallas_call(

time: 89.7 us -> 83 us (0.925)
  Pallas kernels: 87 us -> 79.8 us
    pallas_call x1, Pallas kernels: 87 us -> 79.8 us  [body(): pl.pallas_call(kernel, out_shape=(jax.ShapeDtypeStruct((COL, TOK), BF), j...]
where the time goes in v3:
time: 83 us; the launch traced here: 82.4 us
  Pallas kernels  79.8 us (96%)
  local copies, waits for them, and re-layouts  1.92 us (2%)
    pallas_call x1, Pallas kernels, body(): pl.pallas_call(kernel, out_shape=(jax.ShapeDtypeStruct((COL, TOK), BF), j...  79.8 us
    unnamed x4, local copies, waits for them, and re-layouts  1.92 us

profile of v3, /device:TPU:1, one launch (start us, length us, event | category | flops | bytes accessed | tf_op | source)
XLA Modules:
  0.0 82.4 jit_solution(5639342466457385124)
XLA Ops:
  0.6 79.8 %layer.1 = (bf16[56,64]{1,0:T(8,128)(2,1)}, bf16[56,64]{1,0:T(8,128)(2,1)}) custom-call(bf16[64,3584]{1,0:T(8,128)(2,1)} %tokens_h.1, f32[28,128]{1,0:T(8,128)} %bitcast.13, bf16[56,3584]{1,0:T(8,128)(2,1)} %bitcast.11, f32[1,56]{1,0:T(1,128)} %bitcast.16, bf16[4,1024,128]{2,1,0:T(8,128)(2,1)} %keys_h.1, bf16[4,1024,128]{2,1,0:T(8,128)(2,1)} %values_h.1, ...), custom_call_target="tpu_custom_call" | custom-call | tf_op jit(solution)/shard_map/layer/pallas_call | solution.py:480
  80.5 0.0 copy-start
  80.5 1.3 %copy.15 = bf16[64,56]{0,1:T(8,128)(2,1)} copy(bf16[64,56]{0,1:T(8,128)(2,1)} %bitcast.15) | data formatting | bytes 14336
  81.8 0.0 copy-done
  81.8 0.6 copy.16
Async XLA Ops:
  80.5 1.3 %copy-start = (bf16[56,64]{1,0:T(8,128)(2,1)S(1)}, bf16[56,64]{1,0:T(8,128)(2,1)}, u32[]{:S(2)}) copy-start(bf16[56,64]{1,0:T(8,128)(2,1)} %get-tuple-element.5) | copy-start | bytes 21508

commit v4 on v3

--- a/solution.py
+++ b/solution.py
@@ -21,8 +21,8 @@
 FEAT = D // MP
 PEER = FEAT // COL
 HID = 296
-QUART = 80
-HIDP = QUART * MP
+SHARE = 160
+HIDP = 2 * SHARE
 PK = 32
 LINE = 8
 EPS = 1e-06
@@ -112,6 +112,21 @@
     mine = x // 2 == c
     same_y = yl == yh
 
+    bar = pltpu.get_barrier_semaphore()
+
+    def greet(p, q):
+        pl.semaphore_signal(bar, inc=1, device_id=(p, q), device_id_type=MESH)
+
+    for d in (4, 3, 5, 2, 6, 1, 7, 0):
+        for u, v in ((1, 0), (1, 1), (0, 1), (0, 0)):
+            if d or u or v:
+                greet(32 * lax.rem(yh + u, 2) + LINE * x + lax.rem(z + d, LINE), 2 * lax.rem(yl + v, 2) + c)
+    for i in (2, 1, 3):
+        greet(32 * (1 - yh) + LINE * lax.rem(x + i, 4) + z, m)
+    for i in (6, 2, 5, 7, 1, 3, 4):
+        greet(32 * yh + LINE * lax.rem(x + i % 4, 4) + z, 2 * yl + lax.rem(c + i // 4, 2))
+    greet(s, 2 * (1 - yl) + 1 - c)
+
     pairs = (
         (tokens_h, tokens), (gain_attn_h, gain_attn), (wq_h, wq), (bias_h, bias),
         (keys_h.at[m], keys), (values_h.at[m], values), (wo_h, wo), (gain_ffn_h, gain_ffn),
@@ -120,20 +135,6 @@
     loads = [pltpu.make_async_copy(a, b, in_sem.at[i]) for i, (a, b) in enumerate(pairs)]
     for load in loads:
         load.start()
-
-    bar = pltpu.get_barrier_semaphore()
-
-    def greet(p, q):
-        pl.semaphore_signal(bar, inc=1, device_id=(p, q), device_id_type=MESH)
-
-    for i in range(1, 32):
-        u, v, d = i // 16, (i // 8) % 2, i % 8
-        greet(32 * lax.rem(yh + u, 2) + LINE * x + lax.rem(z + d, LINE), 2 * lax.rem(yl + v, 2) + c)
-    for i in range(1, 8):
-        greet(32 * yh + LINE * lax.rem(x + i % 4, 4) + z, 2 * yl + lax.rem(c + i // 4, 2))
-    for i in range(1, 4):
-        greet(32 * (1 - yh) + LINE * lax.rem(x + i, 4) + z, m)
-    greet(s, 2 * (1 - yl) + 1 - c)
 
     loads[0].wait()
     loads[1].wait()
@@ -279,13 +280,13 @@
 
     low8 = low_lanes(8)
 
-    def collect_x(stage, plane, k, t, stats):
+    def collect_x(stage, plane, k, t, halves, stats):
         tile = pl.ds(128 * t, 128)
 
         def step(i, carry):
             e = far_first(i)
             to_z = lax.rem(z + e, LINE)
-            for half in range(2):
+            for half in halves:
                 j = half * LINE + to_z
                 r = outs[pl.ds(pl.multiple_of(j * COL, 8), 2 * PK), tile]
                 lo, hi = r[0:PK], r[PK : 2 * PK]
@@ -298,7 +299,7 @@
                     b = jnp.concatenate([b[0:24], jnp.where(low8, b[24:PK], both)], axis=0)
                 stage[t, to_z, 2 * half] = a.astype(BF)
                 stage[t, to_z, 2 * half + 1] = b.astype(BF)
-            for g in range(4):
+            for g in [2 * half + i for half in halves for i in range(2)]:
                 to = (32 * yh + LINE * (2 * c + g // 2) + z, 2 * yl + g % 2)
                 local = jnp.logical_and(2 * c + g // 2 == x, g % 2 == c)
                 copy(stage.at[t, to_z, g], plane.at[t, to_z, x], psend.at[k], rrecv.at[k, t, e], *to, local)
@@ -347,9 +348,11 @@
             attend(t, 2 * i, 2)
             return carry
 
-        lax.fori_loop(0, GROUP // 2, two_heads, 0)
-        attend(t, GROUP - 1, 1)
-        collect_x(stage2, plane2, 1, t, True)
+        lax.fori_loop(0, 2, two_heads, 0)
+        collect_x(stage2, plane2, 1, t, (0,), True)
+        attend(t, 4, 2)
+        attend(t, 6, 1)
+        collect_x(stage2, plane2, 1, t, (1,), True)
 
     def join2(chunks, to_z):
         value, levels = merge(chunks, LINE * xb + to_z)
@@ -364,8 +367,8 @@
     on_to_plane(line3, buf3, 2)
 
     def unpacked(x, out):
-        out[pl.ds(0, PK), :] = x[:, 0:64].astype(BF)
-        out[pl.ds(PK, COL - PK), :] = swap(x)[0 : COL - PK, 0:64].astype(BF)
+        out[pl.ds(0, PK), :] = x[:, 0:64]
+        out[pl.ds(PK, COL - PK), :] = swap(x)[0 : COL - PK, 0:64]
 
     unpacked(merged.astype(F32), att_out)
     res_hid = packed(hid_t[...])
@@ -384,6 +387,19 @@
     spread_yz(own4, held4, 3)
     spread_x(held4, buf4, 3)
 
+    def rows_of(core):
+        return pl.ds(pl.multiple_of(core * SHARE, 16), SHARE)
+
+    def put_sums(ref, gate, up, sq):
+        ref[pl.ds(0, SHARE)] = gate.astype(BF)
+        ref[pl.ds(SHARE, SHARE)] = up.astype(BF)
+        ref[pl.ds(2 * SHARE, 16)] = three_rows(sq, 16).astype(BF)
+
+    def add_sums(ref, gate, up, sq):
+        gate = gate + ref[pl.ds(0, SHARE)].astype(F32)
+        up = up + ref[pl.ds(SHARE, SHARE)].astype(F32)
+        return gate, up, sq + jnp.sum(ref[pl.ds(2 * SHARE, 16)].astype(F32), axis=0, keepdims=True)
+
     sqs = []
     for t in range(2):
         tile = pl.ds(128 * t, 128)
@@ -392,39 +408,31 @@
         features = work[pl.ds(0, FEAT), tile].astype(BF)
         gu[0, pl.ds(0, HID), tile] = dot(wg[...], features)
         gu[1, pl.ds(0, HID), tile] = dot(wu[...], features)
-        sq_rows = three_rows(sq, 16).astype(BF)
-        for d in (2, 3, 1):
-            q = lax.rem(m + d, MP)
-            at = pl.multiple_of(q * QUART, 16)
-            gstage[t, d, pl.ds(0, QUART)] = gu[0, pl.ds(at, QUART), tile].astype(BF)
-            gstage[t, d, pl.ds(QUART, QUART)] = gu[1, pl.ds(at, QUART), tile].astype(BF)
-            gstage[t, d, pl.ds(2 * QUART, 16)] = sq_rows
-            remote(gstage.at[t, d], gbuf.at[t, d], asem.at[0, t, d], asem.at[1, t, d], s, q)
+        put_sums(gstage.at[t, 0], gu[0, rows_of(1 - c), tile], gu[1, rows_of(1 - c), tile], sq)
+        remote(gstage.at[t, 0], gbuf.at[t, 0], asem.at[0, t, 0], asem.at[1, t, 0], s, 2 * yl + 1 - c)
         sqs.append(sq)
-    at = pl.multiple_of(m * QUART, 16)
-    own_rows = pl.ds(at, QUART)
+    sums = []
     for t in range(2):
         tile = pl.ds(128 * t, 128)
-        gate, up, sq = gu[0, own_rows, tile], gu[1, own_rows, tile], sqs[t]
-        for d in (1, 3, 2):
-            arrived(gbuf.at[t, d], asem.at[1, t, d])
-            gate += gbuf[t, d, pl.ds(0, QUART)].astype(F32)
-            up += gbuf[t, d, pl.ds(QUART, QUART)].astype(F32)
-            sq += jnp.sum(gbuf[t, d, pl.ds(2 * QUART, 16)].astype(F32), axis=0, keepdims=True)
+        arrived(gbuf.at[t, 0], asem.at[1, t, 0])
+        gate, up, sq = add_sums(gbuf.at[t, 0], gu[0, rows_of(c), tile], gu[1, rows_of(c), tile], sqs[t])
+        put_sums(gstage.at[t, 1], gate, up, sq)
+        remote(gstage.at[t, 1], gbuf.at[t, 1], asem.at[0, t, 1], asem.at[1, t, 1], s, 2 * (1 - yl) + c)
+        sums.append((gate, up, sq))
+    for t in range(2):
+        arrived(gbuf.at[t, 1], asem.at[1, t, 1])
+        gate, up, sq = add_sums(gbuf.at[t, 1], *sums[t])
         factor = lax.rsqrt(sq * (1.0 / D) + EPS)
         gate = gate * factor
         up = up * factor
-        act[t, own_rows] = (gate / (1.0 + jnp.exp(-gate)) * up).astype(BF)
-        for d in (2, 3, 1):
-            part = act.at[t, own_rows]
-            remote(part, part, asem.at[2, t, d], asem.at[3, t, d], s, lax.rem(m + d, MP))
+        act[t, rows_of(c)] = (gate / (1.0 + jnp.exp(-gate)) * up).astype(BF)
+        part = act.at[t, rows_of(c)]
+        remote(part, part, asem.at[0, t, 2], asem.at[1, t, 2], s, 2 * yl + 1 - c)
 
     for t in range(2):
-        for d in (1, 3, 2):
-            rows = pl.ds(pl.multiple_of(lax.rem(m + MP - d, MP) * QUART, 16), QUART)
-            arrived(act.at[t, rows], asem.at[3, t, d])
+        arrived(act.at[t, rows_of(1 - c)], asem.at[1, t, 2])
         outs[pl.ds(0, FEAT), pl.ds(128 * t, 128)] = dot(wd_t[...], act[t])
-        collect_x(stage6, plane6, 4, t, False)
+        collect_x(stage6, plane6, 4, t, (0, 1), False)
     collect_yz(plane6, rel6, held6, 4, lambda chunks, to_z: jnp.sum(chunks, axis=0))
     unpacked(res[...] + jnp.sum(held6[...].astype(F32), axis=0), lay_out)
 
@@ -443,9 +451,9 @@
     arrived(line3.at[pl.ds(0, 7)], zsend.at[2])
     arrived(buf3.at[pl.ds(0, 7)], psend.at[2])
     for t in range(2):
-        for d in range(1, MP):
-            arrived(gstage.at[t, d], asem.at[0, t, d])
-            arrived(act.at[t, own_rows], asem.at[2, t, d])
+        arrived(gstage.at[t, 0], asem.at[0, t, 0])
+        arrived(gstage.at[t, 1], asem.at[0, t, 1])
+        arrived(act.at[t, rows_of(c)], asem.at[0, t, 2])
 
 
 def body(tokens, gain_attn, w_query, query_bias, cache_keys, cache_values, w_out, gain_ffn, w_gate, w_up, w_down):
@@ -471,15 +479,15 @@
         v(owners, BF), v(owners, BF),
         v(halves, BF), v(halves, BF), v(pairs, BF), v(pairs, BF),
         v((2, HIDP, ALL), F32),
-        v((2, MP, 2 * QUART + 16, 128), BF), v((2, MP, 2 * QUART + 16, 128), BF),
+        v((2, 2, 2 * SHARE + 16, 128), BF), v((2, 2, 2 * SHARE + 16, 128), BF),
         v((2, HIDP, 128), BF),
         v((PK, 128), F32),
-        sem((11,)), sem((5,)), sem((5, 2, LINE)), sem((5,)), sem((5, 2)), sem((5, 2, LINE)), sem((4, 2, MP)),
+        sem((11,)), sem((5,)), sem((5, 2, LINE)), sem((5,)), sem((5, 2)), sem((5, 2, LINE)), sem((2, 2, 3)),
     ]
     any_space = pl.BlockSpec(memory_space=pl.ANY)
     attended, layer = pl.pallas_call(
         kernel,
-        out_shape=(jax.ShapeDtypeStruct((COL, TOK), BF), jax.ShapeDtypeStruct((COL, TOK), BF)),
+        out_shape=(jax.ShapeDtypeStruct((COL, TOK), F32), jax.ShapeDtypeStruct((COL, TOK), F32)),
         in_specs=[any_space] * 11,
         out_specs=(pl.BlockSpec(memory_space=pltpu.VMEM), pl.BlockSpec(memory_space=pltpu.VMEM)),
         scratch_shapes=scratch,
@@ -491,7 +499,7 @@
         tokens, gain_attn.reshape(D // 128, 128), w_query.T, query_bias.reshape(1, COL), cache_keys, cache_values,
         w_out.T, gain_ffn.reshape(1, COL), w_gate.T, w_up.T, w_down,
     )
-    return attended.T, layer.T
+    return attended.T.astype(BF), layer.T.astype(BF)
 
 
 def solution(mesh):

time: 83 us -> 84.1 us (1.013); the launches traced: 82.4 us -> 82.5 us
  local copies, waits for them, and re-layouts: 1.92 us -> 0 us
  other arithmetic: 0 us -> 1.37 us
    unnamed x4 -> x0, local copies, waits for them, and re-layouts: 1.92 us -> none
    convert_element_type x0 -> x1, other arithmetic: none -> 1.37 us  [body(): return (attended.T.astype(BF), layer.T.astype(BF))]
where the time goes in v4:
time: 84.1 us; the launch traced here: 82.5 us
  Pallas kernels  80.5 us (96%)
  other arithmetic  1.37 us (2%)
    pallas_call x1, Pallas kernels, body(): pl.pallas_call(kernel, out_shape=(jax.ShapeDtypeStruct((COL, TOK), F32),...  80.5 us

profile of v4, /device:TPU:1, one launch (start us, length us, event | category | flops | bytes accessed | tf_op | source)
XLA Modules:
  0.0 82.5 jit_solution(2950192966708867232)
XLA Ops:
  0.6 80.5 %layer.1 = (f32[56,64]{1,0:T(8,128)}, f32[56,64]{1,0:T(8,128)}) custom-call(bf16[64,3584]{1,0:T(8,128)(2,1)} %tokens_h.1, f32[28,128]{1,0:T(8,128)} %bitcast.15, bf16[56,3584]{1,0:T(8,128)(2,1)} %bitcast.13, f32[1,56]{1,0:T(1,128)} %bitcast.16, bf16[4,1024,128]{2,1,0:T(8,128)(2,1)} %keys_h.1, bf16[4,1024,128]{2,1,0:T(8,128)(2,1)} %values_h.1, ...), custom_call_target="tpu_custom_call" | custom-call | tf_op jit(solution)/shard_map/layer/pallas_call | solution.py:488
  81.1 1.4 %convert_bitcast_fusion = (bf16[64,56]{0,1:T(8,128)(2,1)}, bf16[64,56]{0,1:T(8,128)(2,1)}) fusion(f32[56,64]{1,0:T(8,128)} %get-tuple-element.5, f32[56,64]{1,0:T(8,128)} %get-tuple-element.4), kind=kLoop, calls=%fused_computation | loop fusion | flops 7168 | bytes 43008 | tf_op jit(solution)/shard_map/convert_element_type | solution.py:502

commit v5 on v4

--- a/solution.py
+++ b/solution.py
@@ -97,8 +97,8 @@
     att_out, lay_out,
     tokens, gain_attn, wq, bias, keys, values, wo, gain_ffn, wg, wu, wd,
     normed, value_t, wd_t, hid_t, wo_e, work, outs, lsplit, stage2, stage6,
-    own1, own4, held1, line3, held4, buf1, buf3, buf4, plane2, plane6, rel2, rel6, held2, held6,
-    gu, gstage, gbuf, act, res,
+    own1, own3, own4, held1, line3, held4, buf1, buf3, buf4, plane2, plane6, rel2, rel6, held2, held6,
+    gu, gstage, gbuf, act, res, many,
     in_sem, zsend, zrecv, psend, precv, rrecv, asem,
 ):
     s = lax.axis_index("seq")
@@ -111,6 +111,7 @@
     own_j = LINE * xb + z
     mine = x // 2 == c
     same_y = yl == yh
+    relay = c == 1
 
     bar = pltpu.get_barrier_semaphore()
 
@@ -119,13 +120,15 @@
 
     for d in (4, 3, 5, 2, 6, 1, 7, 0):
         for u, v in ((1, 0), (1, 1), (0, 1), (0, 0)):
-            if d or u or v:
-                greet(32 * lax.rem(yh + u, 2) + LINE * x + lax.rem(z + d, LINE), 2 * lax.rem(yl + v, 2) + c)
+            for w in range(2):
+                if d or u or v or w:
+                    p = 32 * lax.rem(yh + u, 2) + LINE * x + lax.rem(z + d, LINE)
+                    greet(p, 2 * lax.rem(yl + v, 2) + lax.rem(c + w, 2))
     for i in (2, 1, 3):
-        greet(32 * (1 - yh) + LINE * lax.rem(x + i, 4) + z, m)
-    for i in (6, 2, 5, 7, 1, 3, 4):
-        greet(32 * yh + LINE * lax.rem(x + i % 4, 4) + z, 2 * yl + lax.rem(c + i // 4, 2))
-    greet(s, 2 * (1 - yl) + 1 - c)
+        for u in (1, 0):
+            for w in range(2):
+                p = 32 * lax.rem(yh + u, 2) + LINE * lax.rem(x + i, 4) + z
+                greet(p, 2 * yl + lax.rem(c + w, 2))
 
     pairs = (
         (tokens_h, tokens), (gain_attn_h, gain_attn), (wq_h, wq), (bias_h, bias),
@@ -184,52 +187,61 @@
     def spread_yz(own, held, k):
         for d in (4, 3, 5, 2, 6, 1, 7, 0):
             for u in range(2):
-                to = (32 * u + LINE * x + lax.rem(z + d, LINE), 2 * yh + c)
+                to = (32 * u + LINE * x + lax.rem(z + d, LINE), 2 * yh + 1)
                 sems = (zsend.at[k], zrecv.at[k, yl, (LINE - d) % LINE])
-                slot = held.at[yl, z]
+                slot = held.at[yl, z, c]
                 if d:
                     remote(own, slot, *sems, *to)
                 else:
-                    copy(own, slot, *sems, *to, jnp.logical_and(yh == u, same_y))
+                    copy(own, slot, *sems, *to, jnp.logical_and(jnp.logical_and(yh == u, same_y), relay))
 
     def spread_x(held, buf, k):
-        for t in range(2):
-
-            def step(i, carry, t=t):
+        def pass_on():
+            for t in range(2):
+
+                def step(i, carry, t=t):
+                    e = near_first(i)
+                    at = lax.rem(z + e, LINE)
+                    arrived(held.at[t, at], zrecv.at[k, t, e])
+                    for o in (2, 1, 3, 0):
+                        to = (32 * yh + LINE * lax.rem(x + o, 4) + z, 2 * yl + x // 2)
+                        args = (held.at[t, at], buf.at[t, xb, at], psend.at[k], precv.at[k, t], *to)
+                        if o:
+                            remote(*args)
+                        else:
+                            copy(*args, x // 2 == 1)
+                    return carry
+
+                lax.fori_loop(0, LINE, step, 0)
+
+        pl.when(relay)(pass_on)
+
+    def along_line(own, held, k):
+        for d in (4, 3, 5, 2, 6, 1, 7, 0):
+            to = (line + lax.rem(z + d, LINE), 2 * yl + 1)
+            args = (own, held.at[z, c], zsend.at[k], zrecv.at[k, 0, (LINE - d) % LINE], *to)
+            if d:
+                remote(*args)
+            else:
+                copy(*args, relay)
+
+    def on_to_plane(held, buf, k):
+        def pass_on():
+            def step(i, carry):
                 e = near_first(i)
                 at = lax.rem(z + e, LINE)
-                arrived(held.at[t, at], zrecv.at[k, t, e])
-                for o in (2, 1, 3, 0):
-                    to = (32 * yh + LINE * lax.rem(x + o, 4) + z, 2 * yl + x // 2)
-                    args = (held.at[t, at], buf.at[t, 2 * xb + c, at], psend.at[k], precv.at[k, t], *to)
-                    if o:
-                        remote(*args)
-                    else:
-                        copy(*args, mine)
+                arrived(held.at[at], zrecv.at[k, 0, e])
+                for w in range(2):
+                    for d in (6, 2, 5, 7, 1, 3, 4):
+                        p = LINE * lax.rem(here + d, 8) + z
+                        remote(held.at[at, w], buf.at[here, at], psend.at[k], precv.at[k, 0], p, 2 * yl + w)
+                remote(held.at[at, 0], buf.at[here, at], psend.at[k], precv.at[k, 0], s, 2 * yl)
+                pltpu.make_async_copy(held.at[at, 1], buf.at[here, at], precv.at[k, 0]).start()
                 return carry
 
             lax.fori_loop(0, LINE, step, 0)
 
-    def along_line(held, k):
-        for d in (4, 3, 5, 2, 6, 1, 7):
-            remote(held.at[z], held.at[z], zsend.at[k], zrecv.at[k, 0, LINE - d], line + lax.rem(z + d, LINE), m)
-
-    def on_to_plane(held, buf, k):
-        def step(i, carry):
-            e = near_first(i)
-            at = lax.rem(z + e, LINE)
-
-            @pl.when(i > 0)
-            def _():
-                arrived(held.at[at], zrecv.at[k, 0, e])
-
-            for d in range(1, 8):
-                p = LINE * lax.rem(here + d, 8) + z
-                remote(held.at[at], buf.at[here, at], psend.at[k], precv.at[k, 0], p, m)
-            pltpu.make_async_copy(held.at[at], buf.at[here, at], precv.at[k, 0]).start()
-            return carry
-
-        lax.fori_loop(0, LINE, step, 0)
+        pl.when(relay)(pass_on)
 
     own1[...] = packed(q_t).astype(BF)
 
@@ -259,7 +271,7 @@
     for i in (4, 7, 8, 9):
         loads[i].wait()
 
-    pl.semaphore_wait(bar, 42)
+    pl.semaphore_wait(bar, 75)
     spread_yz(own1, held1, 0)
     spread_x(held1, buf1, 0)
 
@@ -267,8 +279,8 @@
         tile = pl.ds(128 * t, 128)
 
         def one(j, total):
-            a = buf[t, 2 * (j // LINE), lax.rem(j, LINE)].astype(F32)
-            b = buf[t, 2 * (j // LINE) + 1, lax.rem(j, LINE)].astype(F32)
+            a = buf[t, j // LINE, lax.rem(j, LINE), 0].astype(F32)
+            b = buf[t, j // LINE, lax.rem(j, LINE), 1].astype(F32)
             lo = jnp.where(low32, a, swap(b))
             hi = jnp.where(low32, swap(a), b)
             at = pl.multiple_of(j * COL, 8)
@@ -297,30 +309,37 @@
                     both = jnp.where(row_ids(8) < 3, lsplit[h0, :, tile], lsplit[h1, :, tile])
                     a = jnp.concatenate([a[0:24], jnp.where(low8, a[24:PK], swap(both))], axis=0)
                     b = jnp.concatenate([b[0:24], jnp.where(low8, b[24:PK], both)], axis=0)
-                stage[t, to_z, 2 * half] = a.astype(BF)
-                stage[t, to_z, 2 * half + 1] = b.astype(BF)
-            for g in [2 * half + i for half in halves for i in range(2)]:
-                to = (32 * yh + LINE * (2 * c + g // 2) + z, 2 * yl + g % 2)
-                local = jnp.logical_and(2 * c + g // 2 == x, g % 2 == c)
-                copy(stage.at[t, to_z, g], plane.at[t, to_z, x], psend.at[k], rrecv.at[k, t, e], *to, local)
+                stage[t, to_z, half, 0] = a.astype(BF)
+                stage[t, to_z, half, 1] = b.astype(BF)
+            for half in halves:
+                to = (32 * yh + LINE * (2 * c + half) + z, 2 * yl + 1)
+                local = jnp.logical_and(2 * c + half == x, relay)
+                copy(stage.at[t, to_z, half], plane.at[t, to_z, x], psend.at[k], rrecv.at[k, t, e], *to, local)
             return carry
 
         lax.fori_loop(0, LINE, step, 0)
 
     def collect_yz(plane, rel, held, k, join):
-        for t in range(2):
-
-            def step(i, carry, t=t):
-                e = far_first(i)
-                to_z = lax.rem(z + e, LINE)
-                arrived(plane.at[t, to_z], rrecv.at[k, t, e])
-                rel[t, to_z] = join(plane[t, to_z].astype(F32), to_z).astype(BF)
-                local = jnp.logical_and(jnp.logical_and(same_y, e == 0), yl == t)
-                to = (32 * yl + LINE * x + to_z, 2 * t + c)
-                copy(rel.at[t, to_z], held.at[2 * z + yh], zsend.at[k], zrecv.at[k, 0, 0], *to, local)
-                return carry
-
-            lax.fori_loop(0, LINE, step, 0)
+        def pass_on():
+            for t in range(2):
+
+                def step(i, carry, t=t):
+                    e = far_first(i)
+                    to_z = lax.rem(z + e, LINE)
+                    arrived(plane.at[t, to_z], rrecv.at[k, t, e])
+                    for w in range(2):
+                        rel[t, to_z, w] = join(plane[t, to_z, :, w].astype(F32), to_z).astype(BF)
+                        args = (rel.at[t, to_z, w], held.at[2 * z + yh], zsend.at[k], zrecv.at[k, 0, 0])
+                        to = (32 * yl + LINE * x + to_z, 2 * t + w)
+                        if w:
+                            copy(*args, *to, jnp.logical_and(jnp.logical_and(same_y, e == 0), yl == t))
+                        else:
+                            remote(*args, *to)
+                    return carry
+
+                lax.fori_loop(0, LINE, step, 0)
+
+        pl.when(relay)(pass_on)
         arrived(held, zrecv.at[k, 0, 0])
 
     scale = HEAD ** (-0.5) * LOG2E
@@ -348,11 +367,9 @@
             attend(t, 2 * i, 2)
             return carry
 
-        lax.fori_loop(0, 2, two_heads, 0)
-        collect_x(stage2, plane2, 1, t, (0,), True)
-        attend(t, 4, 2)
-        attend(t, 6, 1)
-        collect_x(stage2, plane2, 1, t, (1,), True)
+        lax.fori_loop(0, GROUP // 2, two_heads, 0)
+        attend(t, GROUP - 1, 1)
+        collect_x(stage2, plane2, 1, t, (0, 1), True)
 
     def join2(chunks, to_z):
         value, levels = merge(chunks, LINE * xb + to_z)
@@ -361,9 +378,9 @@
 
     collect_yz(plane2, rel2, held2, 1, join2)
     merged = merge(held2[...].astype(F32), own_j)[0].astype(BF)
-    line3[z] = merged
-
-    along_line(line3, 2)
+    own3[...] = merged
+
+    along_line(own3, line3, 2)
     on_to_plane(line3, buf3, 2)
 
     def unpacked(x, out):
@@ -436,20 +453,26 @@
     collect_yz(plane6, rel6, held6, 4, lambda chunks, to_z: jnp.sum(chunks, axis=0))
     unpacked(res[...] + jnp.sum(held6[...].astype(F32), axis=0), lay_out)
 
-    fifteen, most = held2.at[pl.ds(0, 15)], buf3.at[pl.ds(0, 6)]
-    for k in (0, 1, 3, 4):
-        for own, part, whole, sem in ((same_y, fifteen, held2, zsend.at[k]), (mine, most, buf3, psend.at[k])):
-
-            @pl.when(own)
-            def _(part=part, sem=sem):
-                arrived(part, sem)
-
-            @pl.when(jnp.logical_not(own))
-            def _(whole=whole, sem=sem):
-                arrived(whole, sem)
-
-    arrived(line3.at[pl.ds(0, 7)], zsend.at[2])
-    arrived(buf3.at[pl.ds(0, 7)], psend.at[2])
+    def sent(cases, sem):
+        for holds, n in cases:
+
+            @pl.when(holds)
+            def _(n=n):
+                arrived(many.at[pl.ds(0, n)], sem)
+
+    both_true = jnp.logical_and
+    no = jnp.logical_not
+    here_y = both_true(same_y, relay)
+    upper = x // 2 == 1
+    for k in (0, 3):
+        sent(((here_y, 15), (no(here_y), 16)), zsend.at[k])
+        sent(((both_true(relay, upper), 96), (both_true(relay, no(upper)), 128)), psend.at[k])
+    sent(((relay, 7), (no(relay), 8)), zsend.at[2])
+    sent(((relay, 120),), psend.at[2])
+    for k in (1, 4):
+        sent(((here_y, 31), (both_true(relay, no(same_y)), 32)), zsend.at[k])
+        kept = both_true(mine, relay)
+        sent(((kept, 32), (no(kept), 64)), psend.at[k])
     for t in range(2):
         arrived(gstage.at[t, 0], asem.at[0, t, 0])
         arrived(gstage.at[t, 1], asem.at[0, t, 1])
@@ -458,8 +481,9 @@
 
 def body(tokens, gain_attn, w_query, query_bias, cache_keys, cache_values, w_out, gain_ffn, w_gate, w_up, w_down):
     v = pltpu.VMEM
-    one, eight, pairs, halves = (PK, 128), (LINE, PK, 128), (2 * LINE, PK, 128), (2, LINE, PK, 128)
-    chunks, users, owners = (8, LINE, PK, 128), (2, 4, LINE, PK, 128), (2, LINE, 4, PK, 128)
+    one, eight, pairs, halves = (PK, 128), (LINE, 2, PK, 128), (2 * LINE, PK, 128), (2, LINE, 2, PK, 128)
+    chunks, users = (8, LINE, PK, 128), (2, 2, LINE, 2, PK, 128)
+    owners, plane = (2, LINE, 2, 2, PK, 128), (2, LINE, 4, 2, PK, 128)
     sem = pltpu.SemaphoreType.DMA
     scratch = [
         v((TOK, D), BF), v((D // 128, 128), F32), v((COL, D), BF), v((1, COL), F32), v((CTX, HEAD), BF),
@@ -474,14 +498,15 @@
         v((FEAT + 8, ALL), F32),
         v((8, 8, ALL), F32),
         v(owners, BF), v(owners, BF),
-        v(one, BF), v(one, BF), v(halves, BF), v(eight, BF), v(halves, BF),
+        v(one, BF), v(one, BF), v(one, BF), v(halves, BF), v(eight, BF), v(halves, BF),
         v(users, BF), v(chunks, BF), v(users, BF),
-        v(owners, BF), v(owners, BF),
+        v(plane, BF), v(plane, BF),
         v(halves, BF), v(halves, BF), v(pairs, BF), v(pairs, BF),
         v((2, HIDP, ALL), F32),
         v((2, 2, 2 * SHARE + 16, 128), BF), v((2, 2, 2 * SHARE + 16, 128), BF),
         v((2, HIDP, 128), BF),
         v((PK, 128), F32),
+        v((128, PK, 128), BF),
         sem((11,)), sem((5,)), sem((5, 2, LINE)), sem((5,)), sem((5, 2)), sem((5, 2, LINE)), sem((2, 2, 3)),
     ]
     any_space = pl.BlockSpec(memory_space=pl.ANY)

time: 84.1 us -> 84.1 us (level)
  no operation moved by 1% of the time
where the time goes in v5:
time: 84.1 us; the launch traced here: 83.2 us
  Pallas kernels  81.2 us (97%)
  other arithmetic  1.37 us (2%)
    pallas_call x1, Pallas kernels, body(): pl.pallas_call(kernel, out_shape=(jax.ShapeDtypeStruct((COL, TOK), F32),...  81.2 us

profile of v5, /device:TPU:1, one launch (start us, length us, event | category | flops | bytes accessed | tf_op | source)
XLA Modules:
  0.0 83.2 jit_solution(4367569690077081394)
XLA Ops:
  0.6 81.2 %layer.1 = (f32[56,64]{1,0:T(8,128)}, f32[56,64]{1,0:T(8,128)}) custom-call(bf16[64,3584]{1,0:T(8,128)(2,1)} %tokens_h.1, f32[28,128]{1,0:T(8,128)} %bitcast.15, bf16[56,3584]{1,0:T(8,128)(2,1)} %bitcast.13, f32[1,56]{1,0:T(1,128)} %bitcast.16, bf16[4,1024,128]{2,1,0:T(8,128)(2,1)} %keys_h.1, bf16[4,1024,128]{2,1,0:T(8,128)(2,1)} %values_h.1, ...), custom_call_target="tpu_custom_call" | custom-call | tf_op jit(solution)/shard_map/layer/pallas_call | solution.py:513
  81.8 1.4 %convert_bitcast_fusion = (bf16[64,56]{0,1:T(8,128)(2,1)}, bf16[64,56]{0,1:T(8,128)(2,1)}) fusion(f32[56,64]{1,0:T(8,128)} %get-tuple-element.5, f32[56,64]{1,0:T(8,128)} %get-tuple-element.4), kind=kLoop, calls=%fused_computation | loop fusion | flops 7168 | bytes 43008 | tf_op jit(solution)/shard_map/convert_element_type | solution.py:527

commit v6 on v4

--- a/solution.py
+++ b/solution.py
@@ -98,7 +98,7 @@
     tokens, gain_attn, wq, bias, keys, values, wo, gain_ffn, wg, wu, wd,
     normed, value_t, wd_t, hid_t, wo_e, work, outs, lsplit, stage2, stage6,
     own1, own4, held1, line3, held4, buf1, buf3, buf4, plane2, plane6, rel2, rel6, held2, held6,
-    gu, gstage, gbuf, act, res,
+    gu, gstage, gbuf, act, res, many,
     in_sem, zsend, zrecv, psend, precv, rrecv, asem,
 ):
     s = lax.axis_index("seq")
@@ -111,6 +111,7 @@
     own_j = LINE * xb + z
     mine = x // 2 == c
     same_y = yl == yh
+    here_y = jnp.logical_and(same_y, yl == c)
 
     bar = pltpu.get_barrier_semaphore()
 
@@ -119,13 +120,15 @@
 
     for d in (4, 3, 5, 2, 6, 1, 7, 0):
         for u, v in ((1, 0), (1, 1), (0, 1), (0, 0)):
-            if d or u or v:
-                greet(32 * lax.rem(yh + u, 2) + LINE * x + lax.rem(z + d, LINE), 2 * lax.rem(yl + v, 2) + c)
+            for w in range(2):
+                if d or u or v or w:
+                    p = 32 * lax.rem(yh + u, 2) + LINE * x + lax.rem(z + d, LINE)
+                    greet(p, 2 * lax.rem(yl + v, 2) + lax.rem(c + w, 2))
     for i in (2, 1, 3):
-        greet(32 * (1 - yh) + LINE * lax.rem(x + i, 4) + z, m)
-    for i in (6, 2, 5, 7, 1, 3, 4):
-        greet(32 * yh + LINE * lax.rem(x + i % 4, 4) + z, 2 * yl + lax.rem(c + i // 4, 2))
-    greet(s, 2 * (1 - yl) + 1 - c)
+        for u in (1, 0):
+            for w in range(2):
+                p = 32 * lax.rem(yh + u, 2) + LINE * lax.rem(x + i, 4) + z
+                greet(p, 2 * yl + lax.rem(c + w, 2))
 
     pairs = (
         (tokens_h, tokens), (gain_attn_h, gain_attn), (wq_h, wq), (bias_h, bias),
@@ -184,31 +187,29 @@
     def spread_yz(own, held, k):
         for d in (4, 3, 5, 2, 6, 1, 7, 0):
             for u in range(2):
-                to = (32 * u + LINE * x + lax.rem(z + d, LINE), 2 * yh + c)
-                sems = (zsend.at[k], zrecv.at[k, yl, (LINE - d) % LINE])
-                slot = held.at[yl, z]
+                to = (32 * u + LINE * x + lax.rem(z + d, LINE), 2 * yh + yl)
+                sems = (zsend.at[k], zrecv.at[k, 0, (LINE - d) % LINE])
+                slot = held.at[z, c]
                 if d:
                     remote(own, slot, *sems, *to)
                 else:
-                    copy(own, slot, *sems, *to, jnp.logical_and(yh == u, same_y))
+                    copy(own, slot, *sems, *to, jnp.logical_and(yh == u, here_y))
 
     def spread_x(held, buf, k):
-        for t in range(2):
-
-            def step(i, carry, t=t):
-                e = near_first(i)
-                at = lax.rem(z + e, LINE)
-                arrived(held.at[t, at], zrecv.at[k, t, e])
-                for o in (2, 1, 3, 0):
-                    to = (32 * yh + LINE * lax.rem(x + o, 4) + z, 2 * yl + x // 2)
-                    args = (held.at[t, at], buf.at[t, 2 * xb + c, at], psend.at[k], precv.at[k, t], *to)
-                    if o:
-                        remote(*args)
-                    else:
-                        copy(*args, mine)
-                return carry
-
-            lax.fori_loop(0, LINE, step, 0)
+        def step(i, carry):
+            e = near_first(i)
+            at = lax.rem(z + e, LINE)
+            arrived(held.at[at], zrecv.at[k, 0, e])
+            for o in (2, 1, 3, 0):
+                to = (32 * yh + LINE * lax.rem(x + o, 4) + z, 2 * yl + x // 2)
+                args = (held.at[at], buf.at[c, xb, at], psend.at[k], precv.at[k, c], *to)
+                if o:
+                    remote(*args)
+                else:
+                    copy(*args, mine)
+            return carry
+
+        lax.fori_loop(0, LINE, step, 0)
 
     def along_line(held, k):
         for d in (4, 3, 5, 2, 6, 1, 7):
@@ -259,7 +260,7 @@
     for i in (4, 7, 8, 9):
         loads[i].wait()
 
-    pl.semaphore_wait(bar, 42)
+    pl.semaphore_wait(bar, 75)
     spread_yz(own1, held1, 0)
     spread_x(held1, buf1, 0)
 
@@ -267,8 +268,8 @@
         tile = pl.ds(128 * t, 128)
 
         def one(j, total):
-            a = buf[t, 2 * (j // LINE), lax.rem(j, LINE)].astype(F32)
-            b = buf[t, 2 * (j // LINE) + 1, lax.rem(j, LINE)].astype(F32)
+            a = buf[t, j // LINE, lax.rem(j, LINE), 0].astype(F32)
+            b = buf[t, j // LINE, lax.rem(j, LINE), 1].astype(F32)
             lo = jnp.where(low32, a, swap(b))
             hi = jnp.where(low32, swap(a), b)
             at = pl.multiple_of(j * COL, 8)
@@ -297,30 +298,29 @@
                     both = jnp.where(row_ids(8) < 3, lsplit[h0, :, tile], lsplit[h1, :, tile])
                     a = jnp.concatenate([a[0:24], jnp.where(low8, a[24:PK], swap(both))], axis=0)
                     b = jnp.concatenate([b[0:24], jnp.where(low8, b[24:PK], both)], axis=0)
-                stage[t, to_z, 2 * half] = a.astype(BF)
-                stage[t, to_z, 2 * half + 1] = b.astype(BF)
-            for g in [2 * half + i for half in halves for i in range(2)]:
-                to = (32 * yh + LINE * (2 * c + g // 2) + z, 2 * yl + g % 2)
-                local = jnp.logical_and(2 * c + g // 2 == x, g % 2 == c)
-                copy(stage.at[t, to_z, g], plane.at[t, to_z, x], psend.at[k], rrecv.at[k, t, e], *to, local)
+                stage[t, to_z, half, 0] = a.astype(BF)
+                stage[t, to_z, half, 1] = b.astype(BF)
+            for half in halves:
+                to = (32 * yh + LINE * (2 * c + half) + z, 2 * yl + t)
+                local = jnp.logical_and(2 * c + half == x, c == t)
+                copy(stage.at[t, to_z, half], plane.at[to_z, x], psend.at[k], rrecv.at[k, 0, e], *to, local)
             return carry
 
         lax.fori_loop(0, LINE, step, 0)
 
     def collect_yz(plane, rel, held, k, join):
-        for t in range(2):
-
-            def step(i, carry, t=t):
-                e = far_first(i)
-                to_z = lax.rem(z + e, LINE)
-                arrived(plane.at[t, to_z], rrecv.at[k, t, e])
-                rel[t, to_z] = join(plane[t, to_z].astype(F32), to_z).astype(BF)
-                local = jnp.logical_and(jnp.logical_and(same_y, e == 0), yl == t)
-                to = (32 * yl + LINE * x + to_z, 2 * t + c)
-                copy(rel.at[t, to_z], held.at[2 * z + yh], zsend.at[k], zrecv.at[k, 0, 0], *to, local)
-                return carry
-
-            lax.fori_loop(0, LINE, step, 0)
+        def step(i, carry):
+            e = far_first(i)
+            to_z = lax.rem(z + e, LINE)
+            arrived(plane.at[to_z], rrecv.at[k, 0, e])
+            for w in range(2):
+                rel[to_z, w] = join(plane[to_z, :, w].astype(F32), to_z).astype(BF)
+                to = (32 * yl + LINE * x + to_z, 2 * c + w)
+                local = jnp.logical_and(jnp.logical_and(here_y, e == 0), c == w)
+                copy(rel.at[to_z, w], held.at[2 * z + yh], zsend.at[k], zrecv.at[k, 0, 0], *to, local)
+            return carry
+
+        lax.fori_loop(0, LINE, step, 0)
         arrived(held, zrecv.at[k, 0, 0])
 
     scale = HEAD ** (-0.5) * LOG2E
@@ -348,11 +348,9 @@
             attend(t, 2 * i, 2)
             return carry
 
-        lax.fori_loop(0, 2, two_heads, 0)
-        collect_x(stage2, plane2, 1, t, (0,), True)
-        attend(t, 4, 2)
-        attend(t, 6, 1)
-        collect_x(stage2, plane2, 1, t, (1,), True)
+        lax.fori_loop(0, GROUP // 2, two_heads, 0)
+        attend(t, GROUP - 1, 1)
+        collect_x(stage2, plane2, 1, t, (0, 1), True)
 
     def join2(chunks, to_z):
         value, levels = merge(chunks, LINE * xb + to_z)
@@ -436,20 +434,18 @@
     collect_yz(plane6, rel6, held6, 4, lambda chunks, to_z: jnp.sum(chunks, axis=0))
     unpacked(res[...] + jnp.sum(held6[...].astype(F32), axis=0), lay_out)
 
-    fifteen, most = held2.at[pl.ds(0, 15)], buf3.at[pl.ds(0, 6)]
+    def sent(cases, sem):
+        for holds, n in cases:
+
+            @pl.when(holds)
+            def _(n=n):
+                arrived(many.at[pl.ds(0, n)], sem)
+
     for k in (0, 1, 3, 4):
-        for own, part, whole, sem in ((same_y, fifteen, held2, zsend.at[k]), (mine, most, buf3, psend.at[k])):
-
-            @pl.when(own)
-            def _(part=part, sem=sem):
-                arrived(part, sem)
-
-            @pl.when(jnp.logical_not(own))
-            def _(whole=whole, sem=sem):
-                arrived(whole, sem)
-
-    arrived(line3.at[pl.ds(0, 7)], zsend.at[2])
-    arrived(buf3.at[pl.ds(0, 7)], psend.at[2])
+        sent(((here_y, 15), (jnp.logical_not(here_y), 16)), zsend.at[k])
+        sent(((mine, 48), (jnp.logical_not(mine), 64)), psend.at[k])
+    arrived(many.at[pl.ds(0, 7)], zsend.at[2])
+    arrived(many.at[pl.ds(0, 56)], psend.at[2])
     for t in range(2):
         arrived(gstage.at[t, 0], asem.at[0, t, 0])
         arrived(gstage.at[t, 1], asem.at[0, t, 1])
@@ -458,8 +454,9 @@
 
 def body(tokens, gain_attn, w_query, query_bias, cache_keys, cache_values, w_out, gain_ffn, w_gate, w_up, w_down):
     v = pltpu.VMEM
-    one, eight, pairs, halves = (PK, 128), (LINE, PK, 128), (2 * LINE, PK, 128), (2, LINE, PK, 128)
-    chunks, users, owners = (8, LINE, PK, 128), (2, 4, LINE, PK, 128), (2, LINE, 4, PK, 128)
+    one, eight, pairs, halves = (PK, 128), (LINE, PK, 128), (2 * LINE, PK, 128), (LINE, 2, PK, 128)
+    chunks, users = (8, LINE, PK, 128), (2, 2, LINE, 2, PK, 128)
+    owners, plane = (2, LINE, 2, 2, PK, 128), (LINE, 4, 2, PK, 128)
     sem = pltpu.SemaphoreType.DMA
     scratch = [
         v((TOK, D), BF), v((D // 128, 128), F32), v((COL, D), BF), v((1, COL), F32), v((CTX, HEAD), BF),
@@ -474,14 +471,15 @@
         v((FEAT + 8, ALL), F32),
         v((8, 8, ALL), F32),
         v(owners, BF), v(owners, BF),
-        v(one, BF), v(one, BF), v(halves, BF), v(eight, BF), v(halves, BF),
+        v(one, BF), v(one, BF), v(halves, BF), v((LINE, PK, 128), BF), v(halves, BF),
         v(users, BF), v(chunks, BF), v(users, BF),
-        v(owners, BF), v(owners, BF),
+        v(plane, BF), v(plane, BF),
         v(halves, BF), v(halves, BF), v(pairs, BF), v(pairs, BF),
         v((2, HIDP, ALL), F32),
         v((2, 2, 2 * SHARE + 16, 128), BF), v((2, 2, 2 * SHARE + 16, 128), BF),
         v((2, HIDP, 128), BF),
         v((PK, 128), F32),
+        v((64, PK, 128), BF),
         sem((11,)), sem((5,)), sem((5, 2, LINE)), sem((5,)), sem((5, 2)), sem((5, 2, LINE)), sem((2, 2, 3)),
     ]
     any_space = pl.BlockSpec(memory_space=pl.ANY)

time: 84.1 us -> 86.9 us (1.033); the launches traced: 82.5 us -> 86.8 us
  Pallas kernels: 80.5 us -> 84.8 us
    pallas_call x1, Pallas kernels: 80.5 us -> 84.8 us  [body(): pl.pallas_call(kernel, out_shape=(jax.ShapeDtypeStruct((COL, TOK), F32),...]
where the time goes in v6:
time: 86.9 us; the launch traced here: 86.8 us
  Pallas kernels  84.8 us (98%)
  other arithmetic  1.37 us (2%)
    pallas_call x1, Pallas kernels, body(): pl.pallas_call(kernel, out_shape=(jax.ShapeDtypeStruct((COL, TOK), F32),...  84.8 us

profile of v6, /device:TPU:1, one launch (start us, length us, event | category | flops | bytes accessed | tf_op | source)
XLA Modules:
  0.0 86.8 jit_solution(13351727064828024188)
XLA Ops:
  0.6 84.8 %layer.1 = (f32[56,64]{1,0:T(8,128)}, f32[56,64]{1,0:T(8,128)}) custom-call(bf16[64,3584]{1,0:T(8,128)(2,1)} %tokens_h.1, f32[28,128]{1,0:T(8,128)} %bitcast.15, bf16[56,3584]{1,0:T(8,128)(2,1)} %bitcast.13, f32[1,56]{1,0:T(1,128)} %bitcast.16, bf16[4,1024,128]{2,1,0:T(8,128)(2,1)} %keys_h.1, bf16[4,1024,128]{2,1,0:T(8,128)(2,1)} %values_h.1, ...), custom_call_target="tpu_custom_call" | custom-call | tf_op jit(solution)/shard_map/layer/pallas_call | solution.py:486
  85.4 1.4 %convert_bitcast_fusion = (bf16[64,56]{0,1:T(8,128)(2,1)}, bf16[64,56]{0,1:T(8,128)(2,1)}) fusion(f32[56,64]{1,0:T(8,128)} %get-tuple-element.5, f32[56,64]{1,0:T(8,128)} %get-tuple-element.4), kind=kLoop, calls=%fused_computation | loop fusion | flops 7168 | bytes 43008 | tf_op jit(solution)/shard_map/convert_element_type | solution.py:500
